TPU v7x, 256 devices: a 4x2x16 block of a 4x16x16 slice. The times are simulated.
256 devices in a mesh: groups: 2 (over y), blk: 128 (over z, x, core).
Axes of the slice: x: 4, y: 2, z: 16, core: 2. Of those that a mesh axis runs over, the one named last changes fastest.
The devices are a block of a 4x16x16 slice.
Arguments:
- queries: bfloat16 [65536, 2560], P(('groups', 'blk')), parts along dimension 0
- keys: bfloat16 [65536, 2560], P(('groups', 'blk')), parts along dimension 0
- values: bfloat16 [65536, 2560], P(('groups', 'blk')), parts along dimension 0
- out_weight: bfloat16 [64, 2560], replicated, may hold values from -0.125 to 0.125
- latent: float32 [64, 65536], P(None, ('groups', 'blk')), parts along dimension 1, may hold values from -6 to 6
- valid: int32 [256], P('groups'), parts along dimension 0, may hold values from 64 to 256, as said below
- timestep: int32 [2], P('groups'), parts along dimension 0, may hold values from 0 to 9
Outputs:
- velocity: float32 [64, 65536], P(None, ('groups', 'blk')), parts along dimension 1
- latent_next: float32 [64, 65536], P(None, ('groups', 'blk')), parts along dimension 1
There are 2 independent parts, one for each index of `groups`. A program takes and returns all parts, laid end to end along the dimension named above; an argument that names none is the same for every part. Nothing has to cross between parts.
Inputs may be any that keep to these rules, and one draw needn't show every extreme that they name: `valid`: blocks whose index is one less than a multiple of 4 hold between 64 and 256 used tokens; all other blocks are full.
All inputs are finite; a program needn't handle non-finite values.
Results may differ from a plain program's by a relative error of at most 0.0065.
Values may be sent and summed in bfloat16 or wider, within the bound.
No kernel may reach another device: no remote copies, remote signals or barrier semaphores. Data moves between devices by JAX's collectives and lax.ppermute only.
A program may use at most 128 MiB of HBM per device.

v0:
```python
import jax
import jax.numpy as jnp
from jax import lax
from jax.sharding import Mesh
from jax.sharding import PartitionSpec as P

HEADS = 20
HEAD_DIM = 128
LATENT_CH = 64
R_WIN = 2
STEPS = 10
BLK = ("blk_0", "blk_1", "blk_2")
GROUPS_BLK = ("groups", "blk_0", "blk_1", "blk_2")


def shifted(shard, axis, by):
    length = lax.axis_size(axis)
    pairs = [(i, i + by) for i in range(length) if 0 <= i + by < length]
    return lax.ppermute(shard, axis, pairs)


def over_axes(shard, axes):
    for axis in axes:
        shard = lax.psum(shard, axis)
    return shard


def local(queries, keys, values, out_weight, latent, valid, timestep):
    row_count = queries.shape[0]
    own_index = lax.axis_index(BLK)
    block_total = lax.axis_size(BLK)
    score_scale = 1.0 / jnp.sqrt(jnp.float32(HEAD_DIM))
    query_heads = queries.reshape(row_count, HEADS, HEAD_DIM)
    slots = jnp.arange(row_count, dtype=jnp.int32)

    def block_scores(key_value, block):
        inside = (block >= 0) & (block < block_total)
        filled = jnp.where(inside, valid[jnp.clip(block, 0, block_total - 1)], 0)
        key_heads = key_value[0].reshape(row_count, HEADS, HEAD_DIM)
        scores = (
            jnp.einsum("qhd,khd->hqk", query_heads, key_heads, preferred_element_type=jnp.float32)
            * score_scale
        )
        return jnp.where((slots < filled)[None, None, :], scores, jnp.float32(-1e30))

    def weighted(weights, key_value):
        value_heads = key_value[1].reshape(row_count, HEADS, HEAD_DIM)
        return jnp.einsum(
            "hqk,khd->hqd",
            weights.astype(jnp.bfloat16),
            value_heads,
            preferred_element_type=jnp.float32,
        )

    def absorb(carry, key_value, block):
        run_max, run_sum, run_out = carry
        scores = block_scores(key_value, block)
        new_max = jnp.maximum(run_max, jnp.max(scores, axis=-1))
        shrink = jnp.exp(run_max - new_max)
        weights = jnp.exp(scores - new_max[:, :, None])
        run_sum = run_sum * shrink + jnp.sum(weights, axis=-1)
        run_out = run_out * shrink[:, :, None] + weighted(weights, key_value)
        return (new_max, run_sum, run_out)

    own_pair = (keys, values)
    own_scores = block_scores(own_pair, own_index)
    own_max = jnp.max(own_scores, axis=-1)
    own_weights = jnp.exp(own_scores - own_max[:, :, None])
    carry = (own_max, jnp.sum(own_weights, axis=-1), weighted(own_weights, own_pair))
    earlier = own_pair
    following = own_pair
    for distance in range(1, R_WIN + 1):
        earlier = shifted((earlier[0], earlier[1]), BLK, 1)
        following = shifted((following[0], following[1]), BLK, -1)
        carry = absorb(carry, earlier, own_index - distance)
        carry = absorb(carry, following, own_index + distance)
    run_max, run_sum, run_out = carry
    mixed = run_out / run_sum[:, :, None]
    mixed = jnp.transpose(mixed, (1, 0, 2)).reshape(row_count, HEADS * HEAD_DIM)
    used = slots < valid[own_index]
    attn = jnp.where(used[:, None], mixed, 0.0).astype(jnp.bfloat16)
    vel = lax.dot_general(
        out_weight, attn, (((1,), (1,)), ((), ())), preferred_element_type=jnp.float32
    )
    squares = over_axes(jnp.sum(vel * vel), BLK)
    count = jnp.float32(LATENT_CH) * jnp.sum(valid.astype(jnp.float32))
    rms = jnp.sqrt(squares / count + 1e-06)
    velocity = vel / rms
    level = timestep[0].astype(jnp.float32)
    early = 1.0 - level / STEPS
    later = 1.0 - (level + 1.0) / STEPS
    sigma_early = 5.0 * early / (1.0 + 4.0 * early)
    sigma_later = 5.0 * later / (1.0 + 4.0 * later)
    return (velocity, latent + (sigma_later - sigma_early) * velocity)


def solution(mesh):
    split = Mesh(
        mesh.devices.reshape(mesh.shape["groups"], 16, 4, 2), ("groups", "blk_0", "blk_1", "blk_2")
    )
    return jax.shard_map(
        local,
        mesh=split,
        in_specs=(
            P(GROUPS_BLK, None),
            P(GROUPS_BLK, None),
            P(GROUPS_BLK, None),
            P(),
            P(None, GROUPS_BLK),
            P("groups"),
            P("groups"),
        ),
        out_specs=(P(None, GROUPS_BLK), P(None, GROUPS_BLK)),
        check_vma=False,
    )
```

profile of v0, /device:TPU:33, one launch (start us, length us, event | category | flops | bytes accessed | tf_op | source)
XLA Modules:
  0.0 159.9 jit_solution(13057935784155000094)
XLA Ops:
  2.3 22.4 %collective-permute-start.2 = (bf16[256,2560]{0,1:T(8,128)(2,1)S(1)}, bf16[256,2560]{0,1:T(8,128)(2,1)}, u32[]{:S(2)}, u32[]{:S(2)}) collective-permute-start(bf16[256,2560]{0,1:T(8,128)(2,1)S(1)} %copy.26), channel_id=1, source_target_pairs={{1,0},{2,1},{3,2},{4,3},{5,4},{6,5},{7,6},{8,7},{9,8},{10,9},{11,1... | collective-permute-start | bytes 3932168 | tf_op jit(solution)/shard_map/ppermute | solution.py:19
  24.7 2.0 %collective-permute-start = (bf16[256,2560]{0,1:T(8,128)(2,1)S(1)}, bf16[256,2560]{0,1:T(8,128)(2,1)}, u32[]{:S(2)}, u32[]{:S(2)}) collective-permute-start(bf16[256,2560]{0,1:T(8,128)(2,1)S(1)} %copy.26), channel_id=1, source_target_pairs={{0,1},{1,2},{2,3},{3,4},{4,5},{5,6},{6,7},{7,8},{8,9},{9,10},{10,1... | collective-permute-start | bytes 3932168 | tf_op jit(solution)/shard_map/ppermute | solution.py:19
  26.6 2.0 %collective-permute-start.1 = (bf16[256,2560]{1,0:T(8,128)(2,1)}, bf16[256,2560]{1,0:T(8,128)(2,1)}, u32[]{:S(2)}, u32[]{:S(2)}) collective-permute-start(bf16[256,2560]{1,0:T(8,128)(2,1)} %param.9), channel_id=1, source_target_pairs={{0,1},{1,2},{2,3},{3,4},{4,5},{5,6},{6,7},{7,8},{8,9},{9,10},{10,1... | collective-permute-start | bytes 3932168 | tf_op jit(solution)/shard_map/ppermute | solution.py:19
  28.6 3.9 %collective-permute-start.3 = (bf16[256,2560]{1,0:T(8,128)(2,1)}, bf16[256,2560]{1,0:T(8,128)(2,1)}, u32[]{:S(2)}, u32[]{:S(2)}) collective-permute-start(bf16[256,2560]{1,0:T(8,128)(2,1)} %param.9), channel_id=1, source_target_pairs={{1,0},{2,1},{3,2},{4,3},{5,4},{6,5},{7,6},{8,7},{9,8},{10,9},{11,1... | collective-permute-start | bytes 3932168 | tf_op jit(solution)/shard_map/ppermute | solution.py:19
  32.6 2.4 %copy.29 = bf16[256,2560]{0,1:T(8,128)(2,1)} copy(bf16[256,2560]{1,0:T(8,128)(2,1)} %param.9) | data formatting | bytes 2621440 | tf_op args[2]
  42.5 2.9 %fusion.23 = f32[20,256,128]{1,2,0:T(8,128)} fusion(bf16[256,20,128]{0,2,1:T(8,128)(2,1)S(1)} %bitcast.161, f32[20,256,256]{1,2,0:T(8,128)S(1)} %get-tuple-element.26, f32[20,256]{1,0:T(8,128)S(1)} %get-tuple-element.25, pred[256]{0:T(512)(128)(4,1)S(1)} %iota_compare_fusion.4), kind=kOutput, calls=%fused_computation.29 | convolution fusion | flops 340787200 | bytes 9195776 | tf_op jit(solution)/shard_map/hqk,khd->hqd/dot_general | solution.py:48
  48.5 3.7 %collective-permute-start.4 = (bf16[256,2560]{0,1:T(8,128)(2,1)}, bf16[256,2560]{0,1:T(8,128)(2,1)}, u32[]{:S(2)}, u32[]{:S(2)}) collective-permute-start(bf16[256,2560]{0,1:T(8,128)(2,1)} %collective-permute-done), channel_id=1, source_target_pairs={{0,1},{1,2},{2,3},{3,4},{4,5},{5,6},{6,7},{7,8},{8,9},{9,10},{10,1... | collective-permute-start | bytes 3932168 | tf_op jit(solution)/shard_map/ppermute | solution.py:19
  55.3 2.4 %copy.34 = bf16[256,2560]{0,1:T(8,128)(2,1)} copy(bf16[256,2560]{1,0:T(8,128)(2,1)} %collective-permute-done.1) | data formatting | bytes 2621440 | tf_op jit(solution)/shard_map/ppermute | solution.py:19
  57.7 4.4 %collective-permute-start.5 = (bf16[256,2560]{1,0:T(8,128)(2,1)}, bf16[256,2560]{1,0:T(8,128)(2,1)}, u32[]{:S(2)}, u32[]{:S(2)}) collective-permute-start(bf16[256,2560]{1,0:T(8,128)(2,1)} %collective-permute-done.1), channel_id=1, source_target_pairs={{0,1},{1,2},{2,3},{3,4},{4,5},{5,6},{6,7},{7,8},{8,9},{9,10},{10,1... | collective-permute-start | bytes 3932168 | tf_op jit(solution)/shard_map/ppermute | solution.py:19
  63.8 2.0 %collective-permute-start.7 = (bf16[256,2560]{1,0:T(8,128)(2,1)}, bf16[256,2560]{1,0:T(8,128)(2,1)}, u32[]{:S(2)}, u32[]{:S(2)}) collective-permute-start(bf16[256,2560]{1,0:T(8,128)(2,1)} %collective-permute-done.3), channel_id=1, source_target_pairs={{1,0},{2,1},{3,2},{4,3},{5,4},{6,5},{7,6},{8,7},{9,8},{10,9},{11,1... | collective-permute-start | bytes 3932168 | tf_op jit(solution)/shard_map/ppermute | solution.py:19
  65.7 2.7 %fusion.2 = (f32[20,256]{1,0:T(8,128)S(1)}, f32[20,256,256]{1,2,0:T(8,128)S(1)}) fusion(pred[256]{0:T(512)(128)(4,1)S(1)} %iota_compare_fusion.2, bf16[256,20,128]{0,2,1:T(8,128)(2,1)S(1)} %bitcast.154, bf16[256,20,128]{0,2,1:T(8,128)(2,1)} %bitcast.13), kind=kOutput, calls=%fused_computation.12 | convolution fusion | flops 339471360 | bytes 7885056 | tf_op jit(solution)/shard_map/qhd,khd->hqk/dot_general | solution.py:41
  68.4 3.7 %fusion.1 = (f32[20,256]{1,0:T(8,128)S(1)}, f32[20,256,256]{1,2,0:T(8,128)S(1)}) fusion(pred[256]{0:T(512)(128)(4,1)S(1)} %iota_compare_fusion.3, bf16[256,20,128]{0,2,1:T(8,128)(2,1)S(1)} %bitcast.155, bf16[256,20,128]{0,2,1:T(8,128)(2,1)} %bitcast.8), kind=kOutput, calls=%fused_computation.11 | convolution fusion | flops 339471360 | bytes 7885056 | tf_op jit(solution)/shard_map/qhd,khd->hqk/dot_general | solution.py:41
  72.1 2.7 %fusion.4 = (f32[20,256]{1,0:T(8,128)S(1)}, f32[20,256,256]{1,2,0:T(8,128)S(1)}) fusion(pred[256]{0:T(512)(128)(4,1)S(1)} %iota_compare_fusion, bf16[256,20,128]{0,2,1:T(8,128)(2,1)S(1)} %bitcast.156, bf16[256,20,128]{0,2,1:T(8,128)(2,1)} %bitcast.23), kind=kOutput, calls=%fused_computation.14 | convolution fusion | flops 339471360 | bytes 7885056 | tf_op jit(solution)/shard_map/qhd,khd->hqk/dot_general | solution.py:41
  74.8 3.7 %fusion.3 = (f32[20,256]{1,0:T(8,128)S(1)}, f32[20,256,256]{1,2,0:T(8,128)S(1)}) fusion(pred[256]{0:T(512)(128)(4,1)S(1)} %iota_compare_fusion.1, bf16[256,20,128]{0,2,1:T(8,128)(2,1)S(1)} %bitcast.157, bf16[256,20,128]{0,2,1:T(8,128)(2,1)} %bitcast.18), kind=kOutput, calls=%fused_computation.13 | convolution fusion | flops 339471360 | bytes 7885056 | tf_op jit(solution)/shard_map/qhd,khd->hqk/dot_general | solution.py:41
  78.5 2.8 %fusion.7 = (f32[20,256]{1,0:T(8,128)S(1)}, f32[20,256]{1,0:T(8,128)S(1)}) fusion(f32[20,256,256]{1,2,0:T(8,128)S(1)} %get-tuple-element.28, f32[20,256]{1,0:T(8,128)S(1)} %get-tuple-element.12, pred[256]{0:T(512)(128)(4,1)S(1)} %iota_compare_fusion.3, f32[20,256]{1,0:T(8,128)S(1)} %get-tuple-element.11, f32[20,256,256]{1,2,0:T(8,128)S(1)} %get-tuple-element.24, ...), kind=kLoop, calls=%fused_computation.17 | loop fusion | flops 10475520 | bytes 10568192 | tf_op jit(solution)/shard_map/reduce_sum | solution.py:61
  81.4 2.7 %fusion.11 = (f32[20,256]{1,0:T(8,128)S(1)}, f32[20,256]{1,0:T(8,128)S(1)}) fusion(f32[20,256,256]{1,2,0:T(8,128)S(1)} %get-tuple-element.22, f32[20,256]{1,0:T(8,128)S(1)} %get-tuple-element.10, pred[256]{0:T(512)(128)(4,1)S(1)} %iota_compare_fusion.1, f32[20,256]{1,0:T(8,128)S(1)} %get-tuple-element.9, f32[20,256,256]{1,2,0:T(8,128)S(1)} %get-tuple-element.20, ...), kind=kLoop, calls=%fused_computation.21 | loop fusion | flops 10475520 | bytes 10568192 | tf_op jit(solution)/shard_map/reduce_sum | solution.py:61
  84.1 2.8 %fusion.21 = f32[20,256,128]{1,2,0:T(8,128)} fusion(bf16[256,20,128]{0,2,1:T(8,128)(2,1)S(1)} %bitcast.163, f32[20,256,256]{1,2,0:T(8,128)S(1)} %get-tuple-element.28, f32[20,256]{1,0:T(8,128)S(1)} %get-tuple-element.12, pred[256]{0:T(512)(128)(4,1)S(1)} %iota_compare_fusion.3), kind=kOutput, calls=%fused_computation.28 | convolution fusion | flops 340787200 | bytes 9195776 | tf_op jit(solution)/shard_map/hqk,khd->hqd/dot_general | solution.py:48
  88.6 5.5 %fusion.19 = f32[20,256,128]{1,2,0:T(8,128)} fusion(bf16[256,20,128]{0,2,1:T(8,128)(2,1)S(1)} %bitcast.162, f32[20,256,256]{1,2,0:T(8,128)} %copy-done.1, f32[20,256]{1,0:T(8,128)S(1)} %get-tuple-element.11, pred[256]{0:T(512)(128)(4,1)S(1)} %iota_compare_fusion.2), kind=kOutput, calls=%fused_computation.27 | convolution fusion | flops 340787200 | bytes 9195776 | tf_op jit(solution)/shard_map/hqk,khd->hqd/dot_general | solution.py:48
  94.1 2.9 %fusion.17 = f32[20,256,128]{1,2,0:T(8,128)} fusion(bf16[256,20,128]{0,2,1:T(8,128)(2,1)S(1)} %bitcast.164, f32[20,256,256]{1,2,0:T(8,128)S(1)} %bitcast.159, f32[20,256]{1,0:T(8,128)S(1)} %get-tuple-element.10, pred[256]{0:T(512)(128)(4,1)S(1)} %iota_compare_fusion.1), kind=kOutput, calls=%fused_computation.26 | convolution fusion | flops 340787200 | bytes 9195776 | tf_op jit(solution)/shard_map/hqk,khd->hqd/dot_general | solution.py:48
  97.1 2.6 %copy.47 = bf16[256,2560]{0,1:T(8,128)(2,1)} copy(bf16[256,2560]{1,0:T(8,128)(2,1)} %collective-permute-done.7) | data formatting | bytes 2621440 | tf_op jit(solution)/shard_map/ppermute | solution.py:19
  99.6 7.2 %fusion.26 = bf16[256,20,128]{0,2,1:T(8,128)(2,1)S(1)} fusion(f32[20,256,128]{1,2,0:T(8,128)} %fusion.17, f32[20,256,128]{1,2,0:T(8,128)} %fusion.19, f32[20,256,128]{1,2,0:T(8,128)} %fusion.21, f32[20,256,128]{1,2,0:T(8,128)S(1)} %copy-done.6, f32[256,20]{0,1:T(8,128)S(1)} %get-tuple-element.4, f32[256,20]{0,1:T(8,128)S(1)} %get-tuple-element.8, ...), kind=kOutput, calls=%fused_computation.33 | convolution fusion | flops 347340800 | bytes 18473216 | tf_op jit(solution)/shard_map/hqk,khd->hqd/dot_general | solution.py:48
  108.2 28.5 %psum.21 = f32[]{:T(128)} all-reduce(f32[]{:T(128)} %get-tuple-element.29), channel_id=1, replica_groups=mesh['groups'=2,'blk_0'=16,'blk_1'=4,'blk_2'=2] {'blk_0'}, use_global_device_ids=true, to_apply=%region_11.12 | all-reduce | flops 1 | bytes 8 | tf_op jit(solution)/shard_map/psum | solution.py:24
  136.7 8.0 %psum.22 = f32[]{:T(128)} all-reduce(f32[]{:T(128)} %psum.21), channel_id=1, replica_groups=mesh['groups'=2,'blk_0'=16,'blk_1'=4,'blk_2'=2] {'blk_1'}, use_global_device_ids=true, to_apply=%region_12.13 | all-reduce | flops 1 | bytes 8 | tf_op jit(solution)/shard_map/psum | solution.py:24
  144.7 13.9 %psum.23 = f32[]{:T(128)} all-reduce(f32[]{:T(128)} %psum.22), channel_id=1, replica_groups=mesh['groups'=2,'blk_0'=16,'blk_1'=4,'blk_2'=2] {'blk_2'}, use_global_device_ids=true, to_apply=%region_13.14 | all-reduce | flops 1 | bytes 8 | tf_op jit(solution)/shard_map/psum | solution.py:24
  (51 shorter events, 16.0 us)
Async XLA Ops:
  0.6 106.6 %copy-start = (bf16[64,2560]{1,0:T(8,128)(2,1)S(1)}, bf16[64,2560]{1,0:T(8,128)(2,1)}, u32[]{:S(2)}) copy-start(bf16[64,2560]{1,0:T(8,128)(2,1)} %param.10) | copy-start | bytes 983044
  0.6 34.3 %copy-start.8 = (s32[128]{0:T(128)S(1)}, s32[128]{0:T(128)}, u32[]{:S(2)}) copy-start(s32[128]{0:T(128)} %param.12) | copy-start | bytes 1540
  2.3 43.1 %collective-permute-start.2 = (bf16[256,2560]{0,1:T(8,128)(2,1)S(1)}, bf16[256,2560]{0,1:T(8,128)(2,1)}, u32[]{:S(2)}, u32[]{:S(2)}) collective-permute-start(bf16[256,2560]{0,1:T(8,128)(2,1)S(1)} %copy.26), channel_id=1, source_target_pairs={{1,0},{2,1},{3,2},{4,3},{5,4},{6,5},{7,6},{8,7},{9,8},{10,9},{11,1... | collective-permute-start | bytes 3932168 | tf_op jit(solution)/shard_map/ppermute | solution.py:19
  24.7 23.9 %collective-permute-start = (bf16[256,2560]{0,1:T(8,128)(2,1)S(1)}, bf16[256,2560]{0,1:T(8,128)(2,1)}, u32[]{:S(2)}, u32[]{:S(2)}) collective-permute-start(bf16[256,2560]{0,1:T(8,128)(2,1)S(1)} %copy.26), channel_id=1, source_target_pairs={{0,1},{1,2},{2,3},{3,4},{4,5},{5,6},{6,7},{7,8},{8,9},{9,10},{10,1... | collective-permute-start | bytes 3932168 | tf_op jit(solution)/shard_map/ppermute | solution.py:19
  26.6 28.7 %collective-permute-start.1 = (bf16[256,2560]{1,0:T(8,128)(2,1)}, bf16[256,2560]{1,0:T(8,128)(2,1)}, u32[]{:S(2)}, u32[]{:S(2)}) collective-permute-start(bf16[256,2560]{1,0:T(8,128)(2,1)} %param.9), channel_id=1, source_target_pairs={{0,1},{1,2},{2,3},{3,4},{4,5},{5,6},{6,7},{7,8},{8,9},{9,10},{10,1... | collective-permute-start | bytes 3932168 | tf_op jit(solution)/shard_map/ppermute | solution.py:19
  28.6 33.6 %collective-permute-start.3 = (bf16[256,2560]{1,0:T(8,128)(2,1)}, bf16[256,2560]{1,0:T(8,128)(2,1)}, u32[]{:S(2)}, u32[]{:S(2)}) collective-permute-start(bf16[256,2560]{1,0:T(8,128)(2,1)} %param.9), channel_id=1, source_target_pairs={{1,0},{2,1},{3,2},{4,3},{5,4},{6,5},{7,6},{8,7},{9,8},{10,9},{11,1... | collective-permute-start | bytes 3932168 | tf_op jit(solution)/shard_map/ppermute | solution.py:19
  41.1 1.4 copy-start.4
  45.4 26.7 %collective-permute-start.6 = (bf16[256,2560]{0,1:T(8,128)(2,1)}, bf16[256,2560]{0,1:T(8,128)(2,1)}, u32[]{:S(2)}, u32[]{:S(2)}) collective-permute-start(bf16[256,2560]{0,1:T(8,128)(2,1)} %collective-permute-done.2), channel_id=1, source_target_pairs={{1,0},{2,1},{3,2},{4,3},{5,4},{6,5},{7,6},{8,7},{9,8},{10,9},{11,1... | collective-permute-start | bytes 3932168 | tf_op jit(solution)/shard_map/ppermute | solution.py:19
  48.5 26.3 %collective-permute-start.4 = (bf16[256,2560]{0,1:T(8,128)(2,1)}, bf16[256,2560]{0,1:T(8,128)(2,1)}, u32[]{:S(2)}, u32[]{:S(2)}) collective-permute-start(bf16[256,2560]{0,1:T(8,128)(2,1)} %collective-permute-done), channel_id=1, source_target_pairs={{0,1},{1,2},{2,3},{3,4},{4,5},{5,6},{6,7},{7,8},{8,9},{9,10},{10,1... | collective-permute-start | bytes 3932168 | tf_op jit(solution)/shard_map/ppermute | solution.py:19
  57.7 29.2 %collective-permute-start.5 = (bf16[256,2560]{1,0:T(8,128)(2,1)}, bf16[256,2560]{1,0:T(8,128)(2,1)}, u32[]{:S(2)}, u32[]{:S(2)}) collective-permute-start(bf16[256,2560]{1,0:T(8,128)(2,1)} %collective-permute-done.1), channel_id=1, source_target_pairs={{0,1},{1,2},{2,3},{3,4},{4,5},{5,6},{6,7},{7,8},{8,9},{9,10},{10,1... | collective-permute-start | bytes 3932168 | tf_op jit(solution)/shard_map/ppermute | solution.py:19
  63.8 33.3 %collective-permute-start.7 = (bf16[256,2560]{1,0:T(8,128)(2,1)}, bf16[256,2560]{1,0:T(8,128)(2,1)}, u32[]{:S(2)}, u32[]{:S(2)}) collective-permute-start(bf16[256,2560]{1,0:T(8,128)(2,1)} %collective-permute-done.3), channel_id=1, source_target_pairs={{1,0},{2,1},{3,2},{4,3},{5,4},{6,5},{7,6},{8,7},{9,8},{10,9},{11,1... | collective-permute-start | bytes 3932168 | tf_op jit(solution)/shard_map/ppermute | solution.py:19
  68.4 10.1 %copy-start.1 = (f32[20,256,256]{1,2,0:T(8,128)}, f32[20,256,256]{1,2,0:T(8,128)S(1)}, u32[]{:S(2)}) copy-start(f32[20,256,256]{1,2,0:T(8,128)S(1)} %get-tuple-element.24) | copy-start | bytes 15728644
  74.8 6.6 %copy-start.3 = (f32[20,256,256]{1,2,0:T(8,128)}, f32[20,256,256]{1,2,0:T(8,128)S(1)}, u32[]{:S(2)}) copy-start(f32[20,256,256]{1,2,0:T(8,128)S(1)} %get-tuple-element.20) | copy-start | bytes 15728644
  78.5 2.9 %copy-start.2 = (f32[20,256,256]{1,2,0:T(8,128)}, f32[20,256,256]{1,2,0:T(8,128)S(1)}, u32[]{:S(2)}) copy-start(f32[20,256,256]{1,2,0:T(8,128)S(1)} %get-tuple-element.22) | copy-start | bytes 15728644
  81.4 2.7 %copy-start.5 = (bf16[256,2560]{0,1:T(8,128)(2,1)S(1)}, bf16[256,2560]{0,1:T(8,128)(2,1)}, u32[]{:S(2)}) copy-start(bf16[256,2560]{0,1:T(8,128)(2,1)} %copy.34) | copy-start | bytes 3932164
  88.5 5.6 %slice-start = ((s8[5242880]{0:T(1024)(128)(4,1)}), s8[4194304]{0:T(1024)(128)(4,1)S(1)}, s32[]{:S(2)}) async-start(s8[5242880]{0:T(1024)(128)(4,1)} %bitcast.158), calls=%async_computation | async-start | bytes 8388608
  88.6 5.6 %slice-start.1 = ((s8[5242880]{0:T(1024)(128)(4,1)}), s8[1048576]{0:T(1024)(128)(4,1)S(1)}, s32[]{:S(2)}) async-start(s8[5242880]{0:T(1024)(128)(4,1)} %bitcast.158), calls=%async_computation.1 | async-start | bytes 2097152
  97.1 2.6 %copy-start.6 = (f32[20,256,128]{1,2,0:T(8,128)S(1)}, f32[20,256,128]{1,2,0:T(8,128)}, u32[]{:S(2)}) copy-start(f32[20,256,128]{1,2,0:T(8,128)} %fusion.23) | copy-start | bytes 7864324
  106.9 52.4 %copy-start.7 = (f32[64,256]{1,0:T(8,128)S(1)}, f32[64,256]{1,0:T(8,128)}, u32[]{:S(2)}) copy-start(f32[64,256]{1,0:T(8,128)} %param.11) | copy-start | bytes 196612
where the time goes:
time: 161 us; the launch traced here: 160 us
  blocking collectives  50.3 us (31%)
  starting transfers between devices  42.2 us (26%)
  matrix products  36.4 us (23%)
  local copies, waits for them, and re-layouts  14.6 us (9%)
  other arithmetic  9.02 us (6%)
  between operations  6.32 us (4%)
    psum x3, blocking collectives, over_axes(): shard = lax.psum(shard, axis)  50.3 us
    ppermute x8, starting transfers between devices, shifted(): return lax.ppermute(shard, axis, pairs)  42.2 us
    dot_general x5, matrix products, weighted(): jnp.einsum('hqk,khd->hqd', weights.astype(jnp.bfloat16), value_heads, pre...  21.4 us
    dot_general x5, matrix products, block_scores(): jnp.einsum('qhd,khd->hqk', query_heads, key_heads, preferred_element_type...  14 us
    ppermute x4, local copies, waits for them, and re-layouts, shifted(): return lax.ppermute(shard, axis, pairs)  8.18 us
    unnamed x25, local copies, waits for them, and re-layouts  5.73 us
    reduce_sum x2, other arithmetic, absorb(): run_sum = run_sum * shrink + jnp.sum(weights, axis=-1)  5.51 us
  transfers between devices with their start and end apart: 8, of which 1 were waited for; matrix products, arithmetic and copies ran while one was open for 29% of the time, Pallas kernels for 0%

commit v1 on v0

v1 whole, which is shorter than its diff:
```python
import functools
import math

import jax
import jax.numpy as jnp
from jax import lax
from jax.experimental import pallas as pl
from jax.experimental.pallas import tpu as pltpu
from jax.sharding import Mesh
from jax.sharding import PartitionSpec as P


HEADS = 20
HEAD_DIM = 128
LATENT_CH = 64
PAIRS = HEADS // 2
LANES = 2 * LATENT_CH
STEPS = 10
Z_CORE = ("blk_0", "blk_2")
BLK = ("blk_0", "blk_1", "blk_2")
GROUPS_BLK = ("groups", "blk_0", "blk_1", "blk_2")
SCORE_SCALE = math.log2(math.e) / math.sqrt(HEAD_DIM)
LARGEST = 3.3e38


def dot_last(left, right):
    return lax.dot_general(
        left, right, (((1,), (1,)), ((), ())), preferred_element_type=jnp.float32
    )


def dot_plain(left, right):
    return jnp.dot(left, right, preferred_element_type=jnp.float32)


def columns_of(pair, width):
    return pl.ds(pl.multiple_of(pair * width, width), width)


def project_kernel(counts, values, weight, out):
    def one_pair(pair, carry):
        held = values[:, columns_of(pair, 2 * HEAD_DIM)]
        used = lax.broadcasted_iota(jnp.int32, held.shape, 0) < counts[0]
        held = jnp.where(used, held, jnp.zeros_like(held))
        part = weight[:, columns_of(pair, 2 * HEAD_DIM)]
        even = lax.broadcasted_iota(jnp.int32, part.shape, 1) < HEAD_DIM
        zero = jnp.zeros_like(part)
        stacked = jnp.concatenate(
            [jnp.where(even, part, zero), jnp.where(even, zero, part)], axis=0
        )
        projected = jnp.clip(dot_last(held, stacked), -LARGEST, LARGEST)
        out[:, columns_of(pair, LANES)] = projected.astype(jnp.bfloat16)
        return carry

    lax.fori_loop(0, PAIRS, one_pair, 0)


def head_scores(query, keys, pair, side, columns, counts):
    pieces = []
    part = pl.ds(pl.multiple_of(pair * 2 * HEAD_DIM, HEAD_DIM) + side * HEAD_DIM, HEAD_DIM)
    for block, count in zip(keys, counts):
        score = dot_last(query[:, part], block[:, part]) * SCORE_SCALE
        for at in range(0, score.shape[1], LANES):
            piece = score[:, at : at + LANES]
            pieces.append(jnp.where(columns < count - at, piece, jnp.float32(-1e30)))
    return pieces


def row_max(pieces):
    top = jnp.max(functools.reduce(jnp.maximum, pieces), axis=-1, keepdims=True)
    return jnp.broadcast_to(top, pieces[0].shape)


def row_sum(pieces):
    total = jnp.sum(functools.reduce(jnp.add, pieces), axis=-1, keepdims=True)
    return jnp.broadcast_to(total, pieces[0].shape)


def own_kernel(counts, queries, *refs):
    keys, projected = refs[:2], refs[2:4]
    sums, tops, totals = refs[4:]
    rows = queries.shape[0]
    columns = lax.broadcasted_iota(jnp.int32, (rows, LANES), 1)
    block_counts = [counts[block] for block in range(2)]

    def one_pair(pair, carry):
        parts = []
        for side in range(2):
            pieces = head_scores(queries, keys, pair, side, columns, block_counts)
            top = row_max(pieces)
            weights = [jnp.exp2(piece - top) for piece in pieces]
            tops[2 * pair + side] = top
            totals[2 * pair + side] = row_sum(weights)
            rounded = [weight.astype(jnp.bfloat16) for weight in weights]
            half = len(rounded) // 2
            parts.append(
                dot_plain(
                    jnp.concatenate(rounded[:half], axis=1), projected[0][:, columns_of(pair, LANES)]
                )
                + dot_plain(
                    jnp.concatenate(rounded[half:], axis=1), projected[1][:, columns_of(pair, LANES)]
                )
            )
        sums[:, columns_of(pair, LANES)] = jnp.where(columns < LATENT_CH, *parts)
        return carry

    lax.fori_loop(0, PAIRS, one_pair, 0)


def weights_kernel(counts, queries, *refs):
    keys, (sums, tops, totals) = refs[:3], refs[3:6]
    remote, own_sum = refs[6:9], refs[9]
    rows = queries.shape[0]
    columns = lax.broadcasted_iota(jnp.int32, (rows, LANES), 1)
    block_counts = [counts[2 + block] for block in range(3)]
    own_sum[...] = jnp.zeros_like(own_sum)

    def one_pair(pair, carry):
        scales = []
        for side in range(2):
            pieces = head_scores(queries, keys, pair, side, columns, block_counts)
            own_top = tops[2 * pair + side]
            top = jnp.maximum(row_max(pieces), own_top)
            shrink = jnp.exp2(own_top - top)
            weights = [jnp.exp2(piece - top) for piece in pieces]
            share = 1.0 / (row_sum(weights) + totals[2 * pair + side] * shrink)
            per_block = len(weights) // len(remote)
            for at, weight in enumerate(weights):
                block, half = divmod(at, per_block)
                remote[block][2 * pair + side, :, half * LANES : (half + 1) * LANES] = (
                    weight * share
                ).astype(jnp.bfloat16)
            scales.append(shrink * share)
        scale = jnp.where(columns < LATENT_CH, *scales)
        own_sum[...] += sums[:, columns_of(pair, LANES)] * scale
        return carry

    lax.fori_loop(0, PAIRS, one_pair, 0)


def gather_kernel(blocks, finish, *refs):
    shares, values = refs[:blocks], refs[blocks : 2 * blocks]
    start = refs[2 * blocks]
    even_sum = jnp.zeros(start.shape, jnp.float32)
    odd_sum = jnp.zeros(start.shape, jnp.float32)
    for pair in range(PAIRS):
        for block in range(blocks):
            value = values[block][:, pair * LANES : (pair + 1) * LANES]
            even_sum += dot_plain(shares[block][2 * pair], value)
            odd_sum += dot_plain(shares[block][2 * pair + 1], value)
    low = lax.broadcasted_iota(jnp.int32, start.shape, 1) < LATENT_CH
    both = start[...] + jnp.where(low, even_sum, odd_sum)
    if not finish:
        refs[-1][...] = both
        return
    counts, out, squares = refs[-3:]
    both = both + pltpu.roll(both, LATENT_CH, 1)
    vel = jnp.transpose(both)[:LATENT_CH]
    used = lax.broadcasted_iota(jnp.int32, vel.shape, 1) < counts[0]
    vel = jnp.where(used, vel, 0.0)
    out[...] = vel
    square = jnp.sum(vel * vel, axis=0, keepdims=True)
    squares[...] = jnp.broadcast_to(jnp.sum(square, axis=1, keepdims=True), squares.shape)


def call(kernel, counts_first, operands, outs, limit=24):
    here = pl.BlockSpec(memory_space=pltpu.VMEM)
    scalars = pl.BlockSpec(memory_space=pltpu.SMEM)
    operands = [
        x if at == counts_first else pltpu.with_memory_space_constraint(x, pltpu.VMEM)
        for at, x in enumerate(operands)
    ]
    return pl.pallas_call(
        kernel,
        in_specs=[scalars if at == counts_first else here for at in range(len(operands))],
        out_specs=[here] * len(outs),
        out_shape=[pltpu.VMEM(shape, dtype) for shape, dtype in outs],
        compiler_params=pltpu.CompilerParams(vmem_limit_bytes=limit << 20),
    )(*operands)


def project(counts, values, weight):
    rows = values.shape[0]
    outs = [((rows, PAIRS * LANES), jnp.bfloat16)]
    return call(project_kernel, 0, (counts, values, weight), outs)[0]


def own_attention(counts, queries, keys, projected):
    rows = queries.shape[0]
    outs = [((rows, PAIRS * LANES), jnp.float32)] + [((HEADS, rows, LANES), jnp.float32)] * 2
    return call(own_kernel, 0, (counts, queries, *keys, *projected), outs)


def attention_weights(counts, queries, keys, own):
    rows = queries.shape[0]
    outs = [((HEADS, rows, rows), jnp.bfloat16)] * 3 + [((rows, LANES), jnp.float32)]
    return call(weights_kernel, 0, (counts, queries, *keys, *own), outs)


def gather(shares, values, start, counts=None, copies=1):
    rows = start.shape[0]
    blocks = len(shares)
    operands = [*shares, *values, start]
    if counts is None:
        kernel = functools.partial(gather_kernel, blocks, False)
        return call(kernel, -1, operands, [((rows, LANES), jnp.float32)])[0]
    kernel = functools.partial(gather_kernel, blocks, True)
    outs = [((LATENT_CH, rows), jnp.float32), ((copies, LANES), jnp.float32)]
    return call(kernel, len(operands), [*operands, counts], outs)


def exchange(shard, pairs):
    return lax.ppermute(shard, BLK, pairs)


def exchanged_sum(copies, axes):
    gathered = lax.all_to_all(copies, axes, 0, 0, tiled=True)
    return jnp.sum(gathered, axis=0, keepdims=True)


def step(queries, keys, values, out_weight, latent, valid, timestep):
    blocks = lax.axis_size(BLK)
    own = lax.axis_index(BLK)
    near_pairs = [((i + 2) % blocks if i % 2 == 0 else (i - 2) % blocks, i) for i in range(blocks)]
    far_pairs = [((i - 2) % blocks if i % 2 == 0 else (i + 2) % blocks, i) for i in range(blocks)]
    chip_pairs = [(i, i ^ 1) for i in range(blocks)]
    is_odd = own % 2
    partner = own + 1 - 2 * is_odd
    near = own + 2 - 4 * is_odd
    far = own - 2 + 4 * is_odd
    over = own - 1 + 2 * is_odd
    index = jnp.stack([own, partner, near, far, over])
    inside = (index >= 0) & (index < blocks)
    counts = jnp.where(inside, valid[jnp.clip(index, 0, blocks - 1)], 0).astype(jnp.int32)

    keys_near = exchange(keys, near_pairs)
    keys_far = exchange(keys, far_pairs)
    keys_partner = exchange(keys, chip_pairs)
    projected = project(counts, values, out_weight)
    projected_partner = exchange(projected, chip_pairs)
    own = own_attention(
        counts, queries, (keys, keys_partner), (projected, projected_partner)
    )
    keys_near, projected, *own = lax.optimization_barrier((keys_near, projected, *own))
    projected_near = exchange(projected, near_pairs)
    projected_far = exchange(projected, far_pairs)
    keys_over = exchange(keys_near, chip_pairs)
    shares_near, shares_far, shares_over, own_sum = attention_weights(
        counts, queries, (keys_near, keys_far, keys_over), own
    )
    projected_near, own_sum = lax.optimization_barrier((projected_near, own_sum))
    projected_over = exchange(projected_near, chip_pairs)
    most = gather((shares_near,), (projected_near,), own_sum)
    vel, squares = gather(
        (shares_far, shares_over),
        (projected_far, projected_over),
        most,
        counts,
        lax.axis_size(Z_CORE),
    )

    squares = exchanged_sum(squares, Z_CORE)
    copies = jnp.broadcast_to(squares, (lax.axis_size("blk_1"), LANES))
    squares = exchanged_sum(copies, "blk_1")[0, 0]
    count = jnp.float32(LATENT_CH) * jnp.sum(valid.astype(jnp.float32))
    rms = jnp.sqrt(squares / count + 1e-06)
    velocity = vel / rms
    level = timestep[0].astype(jnp.float32)
    early = 1.0 - level / STEPS
    later = 1.0 - (level + 1.0) / STEPS
    sigma_early = 5.0 * early / (1.0 + 4.0 * early)
    sigma_later = 5.0 * later / (1.0 + 4.0 * later)
    return (velocity, latent + (sigma_later - sigma_early) * velocity)


def solution(mesh):
    split = Mesh(
        mesh.devices.reshape(mesh.shape["groups"], 16, 4, 2), ("groups", "blk_0", "blk_1", "blk_2")
    )
    return jax.shard_map(
        step,
        mesh=split,
        in_specs=(
            P(GROUPS_BLK, None),
            P(GROUPS_BLK, None),
            P(GROUPS_BLK, None),
            P(),
            P(None, GROUPS_BLK),
            P("groups"),
            P("groups"),
        ),
        out_specs=(P(None, GROUPS_BLK), P(None, GROUPS_BLK)),
        check_vma=False,
    )
```

time: 161 us -> 102 us (0.63)
  matrix products: 36.4 us -> 0 us
  blocking collectives: 50.3 us -> 15.1 us
  Pallas kernels: 0 us -> 23.2 us
  local copies, waits for them, and re-layouts: 14.6 us -> 4.48 us
  other arithmetic: 9.02 us -> 1.36 us
  starting transfers between devices: 42.2 us -> 49.3 us
  waiting for transfers between devices: 1.11 us -> 5.35 us
  between operations: 6.32 us -> 2.2 us
    psum x3 -> x0, blocking collectives: 50.3 us -> none  [over_axes(): shard = lax.psum(shard, axis)]
    dot_general x11 -> x0, matrix products: 36.4 us -> none  [the longest x5 21.4 us: weighted(): jnp.einsum('hqk,khd->hqd', weights.astype(jnp.bfloat16), value_heads, pre...]
    pallas_call x0 -> x5, Pallas kernels: none -> 23.2 us  [call(): pl.pallas_call(kernel, in_specs=[scalars if at == counts_first else here...]
    all_to_all x0 -> x1, blocking collectives: none -> 15.1 us  [exchanged_sum(): gathered = lax.all_to_all(copies, axes, 0, 0, tiled=True)]
    ppermute x4 -> x0, local copies, waits for them, and re-layouts: 8.18 us -> none  [shifted(): return lax.ppermute(shard, axis, pairs)]
    reduce_sum x4 -> x3, other arithmetic: 7.3 us -> 0.67 us  [the longest x1 0.6 us: step(): count = jnp.float32(LATENT_CH) * jnp.sum(valid.astype(jnp.float32))]
    all_to_all x0 -> x1, starting transfers between devices: none -> 5.65 us  [exchanged_sum(): gathered = lax.all_to_all(copies, axes, 0, 0, tiled=True)]
    unnamed x25 -> x12, local copies, waits for them, and re-layouts: 5.73 us -> 2.31 us
  transfers between devices with their start and end apart: 8 -> 9, of which waited for: 1 -> 5; matrix products, arithmetic and copies ran while one was open for 29% -> 2% of each run, Pallas kernels for 0% -> 21%
where the time goes in v1:
time: 102 us; the launch traced here: 101 us
  starting transfers between devices  49.3 us (48%)
  Pallas kernels  23.2 us (23%)
  blocking collectives  15.1 us (15%)
  waiting for transfers between devices  5.35 us (5%)
  local copies, waits for them, and re-layouts  4.48 us (4%)
  between operations  2.2 us (2%)
  other arithmetic  1.36 us (1%)
    ppermute x8, starting transfers between devices, exchange(): return lax.ppermute(shard, BLK, pairs)  43.6 us
    pallas_call x5, Pallas kernels, call(): pl.pallas_call(kernel, in_specs=[scalars if at == counts_first else here...  23.2 us
    all_to_all x1, blocking collectives, exchanged_sum(): gathered = lax.all_to_all(copies, axes, 0, 0, tiled=True)  15.1 us
    all_to_all x1, starting transfers between devices, exchanged_sum(): gathered = lax.all_to_all(copies, axes, 0, 0, tiled=True)  5.65 us
    ppermute x8, waiting for transfers between devices, exchange(): return lax.ppermute(shard, BLK, pairs)  3.28 us
    unnamed x12, local copies, waits for them, and re-layouts  2.31 us
    all_to_all x1, waiting for transfers between devices, exchanged_sum(): gathered = lax.all_to_all(copies, axes, 0, 0, tiled=True)  2.07 us
  transfers between devices with their start and end apart: 9, of which 5 were waited for; matrix products, arithmetic and copies ran while one was open for 2% of the time, Pallas kernels for 21%

profile of v1, /device:TPU:33, one launch (start us, length us, event | category | flops | bytes accessed | tf_op | source)
XLA Modules:
  0.0 101.0 jit_solution(17720486516183624077)
XLA Ops:
  0.6 20.5 %collective-permute-start.1 = (bf16[256,2560]{1,0:T(8,128)(2,1)}, bf16[256,2560]{1,0:T(8,128)(2,1)}, u32[]{:S(2)}, u32[]{:S(2)}) collective-permute-start(bf16[256,2560]{1,0:T(8,128)(2,1)} %refs_0_.1), channel_id=1, source_target_pairs={{0,1},{1,0},{2,3},{3,2},{4,5},{5,4},{6,7},{7,6},{8,9},{9,8},{10,11... | collective-permute-start | bytes 3932168 | tf_op jit(solution)/shard_map/ppermute | solution.py:213
  21.3 1.4 %gather_fusion = s32[5]{0:T(128)S(1)} fusion(s32[128]{0:T(128)} %param.12, s32[1024]{0:T(1024)S(1)} %pad_clamp_fusion), kind=kCustom, calls=%fused_computation | custom fusion | bytes 60 | tf_op jit(solution)/shard_map/gather | solution.py:234
  22.8 1.3 %copy-done.1 = bf16[256,2560]{1,0:T(8,128)(2,1)S(1)} copy-done((bf16[256,2560]{1,0:T(8,128)(2,1)S(1)}, bf16[256,2560]{1,0:T(8,128)(2,1)}, u32[]{:S(2)}) %copy-start.1) | copy-done | bytes 1310744
  24.1 1.0 copy-done.3
  25.1 2.5 %shard_map.86.refs_2_ = bf16[256,1280]{1,0:T(8,128)(2,1)S(1)} custom-call(s32[5]{0:T(128)S(1)} %and_select_fusion.counts.refs_5_, bf16[256,2560]{1,0:T(8,128)(2,1)S(1)} %copy-done.1, bf16[64,2560]{1,0:T(8,128)(2,1)S(1)} %copy-done.3), custom_call_target="tpu_custom_call" | custom-call | tf_op jit(solution)/shard_map/pallas_call | solution.py:173
  27.6 6.3 %collective-permute-start.2 = (bf16[256,1280]{1,0:T(8,128)(2,1)S(1)}, bf16[256,1280]{1,0:T(8,128)(2,1)S(1)}, u32[]{:S(2)}, u32[]{:S(2)}) collective-permute-start(bf16[256,1280]{1,0:T(8,128)(2,1)S(1)} %shard_map.86.refs_2_), channel_id=1, source_target_pairs={{0,1},{1,0},{2,3},{3,2},{4,5},{5,4},{6,7},{7,6},{8,9},{9,8},{10,11... | collective-permute-start | bytes 1966088 | tf_op jit(solution)/shard_map/ppermute | solution.py:213
  33.8 0.4 collective-permute-start.3
  34.2 1.3 %collective-permute-done.2.refs_3_ = bf16[256,1280]{1,0:T(8,128)(2,1)S(1)} collective-permute-done((bf16[256,1280]{1,0:T(8,128)(2,1)S(1)}, bf16[256,1280]{1,0:T(8,128)(2,1)S(1)}, u32[]{:S(2)}, u32[]{:S(2)}) %collective-permute-start.2) | collective-permute-done | bytes 655392 | tf_op jit(solution)/shard_map/ppermute | solution.py:213
  35.6 8.9 %shard_map.87 = (f32[256,1280]{1,0:T(8,128)S(1)}, f32[20,256,128]{2,1,0:T(8,128)S(1)}, f32[20,256,128]{2,1,0:T(8,128)S(1)}) custom-call(s32[5]{0:T(128)S(1)} %and_select_fusion.counts.refs_5_, bf16[256,2560]{1,0:T(8,128)(2,1)S(1)} %copy-done, bf16[256,2560]{1,0:T(8,128)(2,1)S(1)} %copy-done.2, bf16[256,2560]{1,0:T(8,128)(2,1)} %collective-permute-done.1.refs_1_, ...), custom_call_target="tpu_custom_call" | custom-call | tf_op jit(solution)/shard_map/pallas_call | solution.py:173
  44.5 5.7 %collective-permute-start.4 = (bf16[256,2560]{1,0:T(8,128)(2,1)S(1)}, bf16[256,2560]{1,0:T(8,128)(2,1)S(1)}, u32[]{:S(2)}, u32[]{:S(2)}) collective-permute-start(bf16[256,2560]{1,0:T(8,128)(2,1)S(1)} %collective-permute-done.refs_0_), channel_id=1, source_target_pairs={{0,1},{1,0},{2,3},{3,2},{4,5},{5,4},{6,7},{7,6},{8,9},{9,8},{10,11... | collective-permute-start | bytes 3932168 | tf_op jit(solution)/shard_map/ppermute | solution.py:213
  50.2 5.4 %collective-permute-start.5 = (bf16[256,1280]{1,0:T(8,128)(2,1)S(1)}, bf16[256,1280]{1,0:T(8,128)(2,1)S(1)}, u32[]{:S(2)}, u32[]{:S(2)}) collective-permute-start(bf16[256,1280]{1,0:T(8,128)(2,1)S(1)} %shard_map.86.refs_2_), channel_id=1, source_target_pairs={{126,0},{3,1},{0,2},{5,3},{2,4},{7,5},{4,6},{9,7},{6,8},{11,9},{8,... | collective-permute-start | bytes 1966088 | tf_op jit(solution)/shard_map/ppermute | solution.py:213
  55.7 0.6 collective-permute-done.3.refs_1_
  56.3 8.7 %shard_map.88 = (bf16[20,256,256]{2,1,0:T(8,128)(2,1)S(1)}, bf16[20,256,256]{2,1,0:T(8,128)(2,1)S(1)}, bf16[20,256,256]{2,1,0:T(8,128)(2,1)S(1)}, f32[256,128]{1,0:T(8,128)S(1)}) custom-call(s32[5]{0:T(128)S(1)} %and_select_fusion.counts.refs_5_, bf16[256,2560]{1,0:T(8,128)(2,1)S(1)} %copy-done, bf16[256,2560]{1,0:T(8,128)(2,1)S(1)} %collective-permute-done.refs_0_, ...), custom_call_target="tpu_custom_call" | custom-call | tf_op jit(solution)/shard_map/pallas_call | solution.py:173
  65.0 0.5 collective-permute-done.6.refs_1_
  65.4 5.3 %collective-permute-start.7 = (bf16[256,1280]{1,0:T(8,128)(2,1)S(1)}, bf16[256,1280]{1,0:T(8,128)(2,1)S(1)}, u32[]{:S(2)}, u32[]{:S(2)}) collective-permute-start(bf16[256,1280]{1,0:T(8,128)(2,1)S(1)} %collective-permute-done.6.refs_1_), channel_id=1, source_target_pairs={{0,1},{1,0},{2,3},{3,2},{4,5},{5,4},{6,7},{7,6},{8,9},{9,8},{10,11... | collective-permute-start | bytes 1966088 | tf_op jit(solution)/shard_map/ppermute | solution.py:213
  70.7 0.8 shard_map.89.refs_4_
  71.6 0.9 collective-permute-done.7.refs_3_
  72.5 2.3 %shard_map.90 = (f32[64,256]{1,0:T(8,128)S(1)}, f32[32,128]{1,0:T(8,128)S(1)}) custom-call(bf16[20,256,256]{2,1,0:T(8,128)(2,1)S(1)} %get-tuple-element.25.refs_0_, bf16[20,256,256]{2,1,0:T(8,128)(2,1)S(1)} %get-tuple-element.26.refs_1_, bf16[256,1280]{1,0:T(8,128)(2,1)S(1)} %collective-permute-done.5.refs_2_, ...), custom_call_target="tpu_custom_call" | custom-call | tf_op jit(solution)/shard_map/pallas_call | solution.py:173
  74.7 15.1 %all_to_all.15 = f32[32,1,128]{2,1,0:T(1,128)S(1)} all-to-all(f32[32,1,128]{2,1,0:T(1,128)S(1)} %bitcast.20), channel_id=1, replica_groups=mesh['groups'=2,'blk_0'=16,'blk_1'=4,'blk_2'=2] {'blk_0','blk_2'}, dimensions={0} | all-to-all | bytes 32768 | tf_op jit(solution)/shard_map/all_to_all | solution.py:217
  89.9 0.6 broadcast_in_dim.6
  90.5 5.7 %all-to-all-start.1 = ((f32[4,1,128]{2,1,0:T(1,128)}), f32[4,1,128]{2,1,0:T(1,128)S(1)}, u32[]{:S(2)}, u32[]{:S(2)}) async-start(f32[4,1,128]{2,1,0:T(1,128)} %broadcast_in_dim.6), calls=%async_computation.1 | async-start | bytes 4096 | tf_op jit(solution)/shard_map/all_to_all | solution.py:217
  96.1 0.6 convert_reduce_fusion
  98.1 2.1 %all-to-all-done.1 = f32[4,1,128]{2,1,0:T(1,128)S(1)} async-done(((f32[4,1,128]{2,1,0:T(1,128)}), f32[4,1,128]{2,1,0:T(1,128)S(1)}, u32[]{:S(2)}, u32[]{:S(2)}) %all-to-all-start.1) | async-done | bytes 2080 | tf_op jit(solution)/shard_map/all_to_all | solution.py:217
  100.3 0.7 multiply_add_fusion
  (23 shorter events, 0.3 us)
Async XLA Ops:
  0.6 34.9 %collective-permute-start.1 = (bf16[256,2560]{1,0:T(8,128)(2,1)}, bf16[256,2560]{1,0:T(8,128)(2,1)}, u32[]{:S(2)}, u32[]{:S(2)}) collective-permute-start(bf16[256,2560]{1,0:T(8,128)(2,1)} %refs_0_.1), channel_id=1, source_target_pairs={{0,1},{1,0},{2,3},{3,2},{4,5},{5,4},{6,7},{7,6},{8,9},{9,8},{10,11... | collective-permute-start | bytes 3932168 | tf_op jit(solution)/shard_map/ppermute | solution.py:213
  21.2 23.4 %collective-permute-start = (bf16[256,2560]{1,0:T(8,128)(2,1)}, bf16[256,2560]{1,0:T(8,128)(2,1)S(1)}, u32[]{:S(2)}, u32[]{:S(2)}) collective-permute-start(bf16[256,2560]{1,0:T(8,128)(2,1)} %refs_0_.1), channel_id=1, source_target_pairs={{2,0},{127,1},{4,2},{1,3},{6,4},{3,5},{8,6},{5,7},{10,8},{7,9},{12... | collective-permute-start | bytes 3932168 | tf_op jit(solution)/shard_map/ppermute | solution.py:213
  21.3 14.3 %copy-start = (bf16[256,2560]{1,0:T(8,128)(2,1)S(1)}, bf16[256,2560]{1,0:T(8,128)(2,1)}, u32[]{:S(2)}) copy-start(bf16[256,2560]{1,0:T(8,128)(2,1)} %queries.3) | copy-start | bytes 3932164
  22.8 1.3 %copy-start.1 = (bf16[256,2560]{1,0:T(8,128)(2,1)S(1)}, bf16[256,2560]{1,0:T(8,128)(2,1)}, u32[]{:S(2)}) copy-start(bf16[256,2560]{1,0:T(8,128)(2,1)} %values.1) | copy-start | bytes 3932164
  24.1 1.0 copy-start.3
  25.1 8.7 %copy-start.2 = (bf16[256,2560]{1,0:T(8,128)(2,1)S(1)}, bf16[256,2560]{1,0:T(8,128)(2,1)}, u32[]{:S(2)}) copy-start(bf16[256,2560]{1,0:T(8,128)(2,1)} %refs_0_.1) | copy-start | bytes 3932164
  27.6 8.0 %collective-permute-start.2 = (bf16[256,1280]{1,0:T(8,128)(2,1)S(1)}, bf16[256,1280]{1,0:T(8,128)(2,1)S(1)}, u32[]{:S(2)}, u32[]{:S(2)}) collective-permute-start(bf16[256,1280]{1,0:T(8,128)(2,1)S(1)} %shard_map.86.refs_2_), channel_id=1, source_target_pairs={{0,1},{1,0},{2,3},{3,2},{4,5},{5,4},{6,7},{7,6},{8,9},{9,8},{10,11... | collective-permute-start | bytes 1966088 | tf_op jit(solution)/shard_map/ppermute | solution.py:213
  33.8 22.5 %collective-permute-start.3 = (bf16[256,2560]{1,0:T(8,128)(2,1)S(1)}, bf16[256,2560]{1,0:T(8,128)(2,1)S(1)}, u32[]{:S(2)}, u32[]{:S(2)}) collective-permute-start(bf16[256,2560]{1,0:T(8,128)(2,1)S(1)} %copy-done.2), channel_id=1, source_target_pairs={{126,0},{3,1},{0,2},{5,3},{2,4},{7,5},{4,6},{9,7},{6,8},{11,9},{8,... | collective-permute-start | bytes 3932168 | tf_op jit(solution)/shard_map/ppermute | solution.py:213
  44.5 11.8 %collective-permute-start.4 = (bf16[256,2560]{1,0:T(8,128)(2,1)S(1)}, bf16[256,2560]{1,0:T(8,128)(2,1)S(1)}, u32[]{:S(2)}, u32[]{:S(2)}) collective-permute-start(bf16[256,2560]{1,0:T(8,128)(2,1)S(1)} %collective-permute-done.refs_0_), channel_id=1, source_target_pairs={{0,1},{1,0},{2,3},{3,2},{4,5},{5,4},{6,7},{7,6},{8,9},{9,8},{10,11... | collective-permute-start | bytes 3932168 | tf_op jit(solution)/shard_map/ppermute | solution.py:213
  50.2 15.2 %collective-permute-start.6 = (bf16[256,1280]{1,0:T(8,128)(2,1)S(1)}, bf16[256,1280]{1,0:T(8,128)(2,1)S(1)}, u32[]{:S(2)}, u32[]{:S(2)}) collective-permute-start(bf16[256,1280]{1,0:T(8,128)(2,1)S(1)} %shard_map.86.refs_2_), channel_id=1, source_target_pairs={{2,0},{127,1},{4,2},{1,3},{6,4},{3,5},{8,6},{5,7},{10,8},{7,9},{12... | collective-permute-start | bytes 1966088 | tf_op jit(solution)/shard_map/ppermute | solution.py:213
  50.2 21.3 %collective-permute-start.5 = (bf16[256,1280]{1,0:T(8,128)(2,1)S(1)}, bf16[256,1280]{1,0:T(8,128)(2,1)S(1)}, u32[]{:S(2)}, u32[]{:S(2)}) collective-permute-start(bf16[256,1280]{1,0:T(8,128)(2,1)S(1)} %shard_map.86.refs_2_), channel_id=1, source_target_pairs={{126,0},{3,1},{0,2},{5,3},{2,4},{7,5},{4,6},{9,7},{6,8},{11,9},{8,... | collective-permute-start | bytes 1966088 | tf_op jit(solution)/shard_map/ppermute | solution.py:213
  65.4 7.0 %collective-permute-start.7 = (bf16[256,1280]{1,0:T(8,128)(2,1)S(1)}, bf16[256,1280]{1,0:T(8,128)(2,1)S(1)}, u32[]{:S(2)}, u32[]{:S(2)}) collective-permute-start(bf16[256,1280]{1,0:T(8,128)(2,1)S(1)} %collective-permute-done.6.refs_1_), channel_id=1, source_target_pairs={{0,1},{1,0},{2,3},{3,2},{4,5},{5,4},{6,7},{7,6},{8,9},{9,8},{10,11... | collective-permute-start | bytes 1966088 | tf_op jit(solution)/shard_map/ppermute | solution.py:213
  72.5 23.7 %copy-start.4 = (s32[128]{0:T(128)S(1)}, s32[128]{0:T(128)}, u32[]{:S(2)}) copy-start(s32[128]{0:T(128)} %param.12) | copy-start | bytes 1540
  72.5 27.9 %copy-start.5 = (f32[64,256]{1,0:T(8,128)S(1)}, f32[64,256]{1,0:T(8,128)}, u32[]{:S(2)}) copy-start(f32[64,256]{1,0:T(8,128)} %param.11) | copy-start | bytes 196612
  90.5 9.7 %all-to-all-start.1 = ((f32[4,1,128]{2,1,0:T(1,128)}), f32[4,1,128]{2,1,0:T(1,128)S(1)}, u32[]{:S(2)}, u32[]{:S(2)}) async-start(f32[4,1,128]{2,1,0:T(1,128)} %broadcast_in_dim.6), calls=%async_computation.1 | async-start | bytes 4096 | tf_op jit(solution)/shard_map/all_to_all | solution.py:217

commit v2 on v1

--- a/solution.py
+++ b/solution.py
@@ -241,7 +241,7 @@
     own = own_attention(
         counts, queries, (keys, keys_partner), (projected, projected_partner)
     )
-    keys_near, projected, *own = lax.optimization_barrier((keys_near, projected, *own))
+    projected, *own = lax.optimization_barrier((projected, *own))
     projected_near = exchange(projected, near_pairs)
     projected_far = exchange(projected, far_pairs)
     keys_over = exchange(keys_near, chip_pairs)
@@ -251,17 +251,23 @@
     projected_near, own_sum = lax.optimization_barrier((projected_near, own_sum))
     projected_over = exchange(projected_near, chip_pairs)
     most = gather((shares_near,), (projected_near,), own_sum)
+    most = gather((shares_far,), (projected_far,), most)
     vel, squares = gather(
-        (shares_far, shares_over),
-        (projected_far, projected_over),
+        (shares_over,),
+        (projected_over,),
         most,
         counts,
-        lax.axis_size(Z_CORE),
-    )
-
-    squares = exchanged_sum(squares, Z_CORE)
-    copies = jnp.broadcast_to(squares, (lax.axis_size("blk_1"), LANES))
-    squares = exchanged_sum(copies, "blk_1")[0, 0]
+        1,
+    )
+
+    columns = lax.axis_size("blk_1")
+    moved = [
+        lax.ppermute(squares, "blk_1", [(i, (i + by) % columns) for i in range(columns)])
+        for by in range(1, columns)
+    ]
+    squares = functools.reduce(jnp.add, moved, squares)
+    copies = jnp.broadcast_to(squares, (lax.axis_size(Z_CORE), LANES))
+    squares = exchanged_sum(copies, Z_CORE)[0, 0]
     count = jnp.float32(LATENT_CH) * jnp.sum(valid.astype(jnp.float32))
     rms = jnp.sqrt(squares / count + 1e-06)
     velocity = vel / rms

time: 102 us -> 110 us (1.078)
  waiting for transfers between devices: 5.35 us -> 23.7 us
  blocking collectives: 15.1 us -> 0 us
  starting transfers between devices: 49.3 us -> 54.4 us
    all_to_all x1 -> x0, blocking collectives: 15.1 us -> none  [exchanged_sum(): gathered = lax.all_to_all(copies, axes, 0, 0, tiled=True)]
    all_to_all x1, waiting for transfers between devices: 2.07 us -> 10.1 us  [exchanged_sum(): gathered = lax.all_to_all(copies, axes, 0, 0, tiled=True)]
    ppermute x8, waiting for transfers between devices: 3.28 us -> 9.62 us  [exchange(): return lax.ppermute(shard, BLK, pairs)]
    ppermute x0 -> x3, waiting for transfers between devices: none -> 3.92 us  [step(): lax.ppermute(squares, 'blk_1', [(i, (i + by) % columns) for i in range(co...]
    all_to_all x1, starting transfers between devices: 5.65 us -> 7.72 us  [exchanged_sum(): gathered = lax.all_to_all(copies, axes, 0, 0, tiled=True)]
    ppermute x8, starting transfers between devices: 43.6 us -> 45.2 us  [exchange(): return lax.ppermute(shard, BLK, pairs)]
    ppermute x0 -> x3, starting transfers between devices: none -> 1.5 us  [step(): lax.ppermute(squares, 'blk_1', [(i, (i + by) % columns) for i in range(co...]
    pallas_call x5 -> x6, Pallas kernels: 23.2 us -> 23.4 us  [call(): pl.pallas_call(kernel, in_specs=[scalars if at == counts_first else here...]
  transfers between devices with their start and end apart: 9 -> 12, of which waited for: 5 -> 6; matrix products, arithmetic and copies ran while one was open for 2% -> 2% of each run, Pallas kernels for 21% -> 20%
where the time goes in v2:
time: 110 us
  starting transfers between devices  54.4 us (49%)
  waiting for transfers between devices  23.7 us (22%)
  Pallas kernels  23.4 us (21%)
  local copies, waits for them, and re-layouts  4.52 us (4%)
  between operations  2.28 us (2%)
  other arithmetic  1.32 us (1%)
    ppermute x8, starting transfers between devices, exchange(): return lax.ppermute(shard, BLK, pairs)  45.2 us
    pallas_call x6, Pallas kernels, call(): pl.pallas_call(kernel, in_specs=[scalars if at == counts_first else here...  23.4 us
    all_to_all x1, waiting for transfers between devices, exchanged_sum(): gathered = lax.all_to_all(copies, axes, 0, 0, tiled=True)  10.1 us
    ppermute x8, waiting for transfers between devices, exchange(): return lax.ppermute(shard, BLK, pairs)  9.62 us
    all_to_all x1, starting transfers between devices, exchanged_sum(): gathered = lax.all_to_all(copies, axes, 0, 0, tiled=True)  7.72 us
    ppermute x3, waiting for transfers between devices, step(): lax.ppermute(squares, 'blk_1', [(i, (i + by) % columns) for i in range(co...  3.92 us
    unnamed x12, local copies, waits for them, and re-layouts  2.32 us
  transfers between devices with their start and end apart: 12, of which 6 were waited for; matrix products, arithmetic and copies ran while one was open for 2% of the time, Pallas kernels for 20%

profile of v2, /device:TPU:33, one launch (start us, length us, event | category | flops | bytes accessed | tf_op | source)
XLA Modules:
  0.0 109.6 jit_solution(12638460331934002092)
XLA Ops:
  0.6 2.3 %collective-permute-start = (bf16[256,2560]{1,0:T(8,128)(2,1)}, bf16[256,2560]{1,0:T(8,128)(2,1)S(1)}, u32[]{:S(2)}, u32[]{:S(2)}) collective-permute-start(bf16[256,2560]{1,0:T(8,128)(2,1)} %refs_0_.1), channel_id=1, source_target_pairs={{2,0},{127,1},{4,2},{1,3},{6,4},{3,5},{8,6},{5,7},{10,8},{7,9},{12... | collective-permute-start | bytes 3932168 | tf_op jit(solution)/shard_map/ppermute | solution.py:213
  2.9 24.2 %collective-permute-start.3 = (bf16[256,2560]{1,0:T(8,128)(2,1)}, bf16[256,2560]{1,0:T(8,128)(2,1)}, u32[]{:S(2)}, u32[]{:S(2)}) collective-permute-start(bf16[256,2560]{1,0:T(8,128)(2,1)} %refs_0_.1), channel_id=1, source_target_pairs={{0,1},{1,0},{2,3},{3,2},{4,5},{5,4},{6,7},{7,6},{8,9},{9,8},{10,11... | collective-permute-start | bytes 3932168 | tf_op jit(solution)/shard_map/ppermute | solution.py:213
  27.3 1.4 %gather_fusion = s32[5]{0:T(128)S(1)} fusion(s32[128]{0:T(128)} %param.12, s32[1024]{0:T(1024)S(1)} %pad_clamp_fusion), kind=kCustom, calls=%fused_computation | custom fusion | bytes 60 | tf_op jit(solution)/shard_map/gather | solution.py:234
  28.8 1.3 %copy-done.1 = bf16[256,2560]{1,0:T(8,128)(2,1)S(1)} copy-done((bf16[256,2560]{1,0:T(8,128)(2,1)S(1)}, bf16[256,2560]{1,0:T(8,128)(2,1)}, u32[]{:S(2)}) %copy-start.1) | copy-done | bytes 1310744
  30.1 1.0 copy-done.3
  31.1 2.5 %shard_map.86.refs_2_ = bf16[256,1280]{1,0:T(8,128)(2,1)S(1)} custom-call(s32[5]{0:T(128)S(1)} %and_select_fusion.counts.refs_3_, bf16[256,2560]{1,0:T(8,128)(2,1)S(1)} %copy-done.1, bf16[64,2560]{1,0:T(8,128)(2,1)S(1)} %copy-done.3), custom_call_target="tpu_custom_call" | custom-call | tf_op jit(solution)/shard_map/pallas_call | solution.py:173
  34.2 8.6 %collective-permute-done.refs_0_ = bf16[256,2560]{1,0:T(8,128)(2,1)S(1)} collective-permute-done((bf16[256,2560]{1,0:T(8,128)(2,1)}, bf16[256,2560]{1,0:T(8,128)(2,1)S(1)}, u32[]{:S(2)}, u32[]{:S(2)}) %collective-permute-start) | collective-permute-done | bytes 1310752 | tf_op jit(solution)/shard_map/ppermute | solution.py:213
  42.9 7.1 %collective-permute-start.2 = (bf16[256,2560]{1,0:T(8,128)(2,1)S(1)}, bf16[256,2560]{1,0:T(8,128)(2,1)S(1)}, u32[]{:S(2)}, u32[]{:S(2)}) collective-permute-start(bf16[256,2560]{1,0:T(8,128)(2,1)S(1)} %collective-permute-done.refs_0_), channel_id=1, source_target_pairs={{0,1},{1,0},{2,3},{3,2},{4,5},{5,4},{6,7},{7,6},{8,9},{9,8},{10,11... | collective-permute-start | bytes 3932168 | tf_op jit(solution)/shard_map/ppermute | solution.py:213
  49.9 8.9 %shard_map.87 = (f32[256,1280]{1,0:T(8,128)S(1)}, f32[20,256,128]{2,1,0:T(8,128)S(1)}, f32[20,256,128]{2,1,0:T(8,128)S(1)}) custom-call(s32[5]{0:T(128)S(1)} %and_select_fusion.counts.refs_3_, bf16[256,2560]{1,0:T(8,128)(2,1)S(1)} %copy-done, bf16[256,2560]{1,0:T(8,128)(2,1)S(1)} %copy-done.2, bf16[256,2560]{1,0:T(8,128)(2,1)} %collective-permute-done.3.refs_1_, ...), custom_call_target="tpu_custom_call" | custom-call | tf_op jit(solution)/shard_map/pallas_call | solution.py:173
  59.0 5.5 %collective-permute-start.7 = (bf16[256,1280]{1,0:T(8,128)(2,1)S(1)}, bf16[256,1280]{1,0:T(8,128)(2,1)S(1)}, u32[]{:S(2)}, u32[]{:S(2)}) collective-permute-start(bf16[256,1280]{1,0:T(8,128)(2,1)S(1)} %shard_map.86.refs_2_), channel_id=1, source_target_pairs={{126,0},{3,1},{0,2},{5,3},{2,4},{7,5},{4,6},{9,7},{6,8},{11,9},{8,... | collective-permute-start | bytes 1966088 | tf_op jit(solution)/shard_map/ppermute | solution.py:213
  64.6 8.7 %shard_map.88 = (bf16[20,256,256]{2,1,0:T(8,128)(2,1)S(1)}, bf16[20,256,256]{2,1,0:T(8,128)(2,1)S(1)}, bf16[20,256,256]{2,1,0:T(8,128)(2,1)S(1)}, f32[256,128]{1,0:T(8,128)S(1)}) custom-call(s32[5]{0:T(128)S(1)} %and_select_fusion.counts.refs_3_, bf16[256,2560]{1,0:T(8,128)(2,1)S(1)} %copy-done, bf16[256,2560]{1,0:T(8,128)(2,1)S(1)} %collective-permute-done.refs_0_, ...), custom_call_target="tpu_custom_call" | custom-call | tf_op jit(solution)/shard_map/pallas_call | solution.py:173
  73.3 1.0 collective-permute-done.5.refs_1_
  74.2 5.3 %collective-permute-start.6 = (bf16[256,1280]{1,0:T(8,128)(2,1)S(1)}, bf16[256,1280]{1,0:T(8,128)(2,1)S(1)}, u32[]{:S(2)}, u32[]{:S(2)}) collective-permute-start(bf16[256,1280]{1,0:T(8,128)(2,1)S(1)} %collective-permute-done.5.refs_1_), channel_id=1, source_target_pairs={{0,1},{1,0},{2,3},{3,2},{4,5},{5,4},{6,7},{7,6},{8,9},{9,8},{10,11... | collective-permute-start | bytes 1966088 | tf_op jit(solution)/shard_map/ppermute | solution.py:213
  80.2 0.8 shard_map.89.refs_2_
  81.0 0.8 shard_map.90.refs_2_
  81.9 1.6 %shard_map.91 = (f32[64,256]{1,0:T(8,128)S(1)}, f32[1,128]{1,0:T(1,128)S(1)}) custom-call(bf16[20,256,256]{2,1,0:T(8,128)(2,1)S(1)} %get-tuple-element.23.refs_0_, bf16[256,1280]{1,0:T(8,128)(2,1)S(1)} %collective-permute-done.6.refs_1_, f32[256,128]{1,0:T(8,128)S(1)} %shard_map.90.refs_2_, s32[5]{0:T(128)S(1)} %and_select_fusion.counts.refs_3_), custom_call_target="tpu_custom_call" | custom-call | tf_op jit(solution)/shard_map/pallas_call | solution.py:173
  83.6 1.4 %collective-permute-start.8 = (f32[1,128]{1,0:T(1,128)S(1)}, f32[1,128]{1,0:T(1,128)S(1)}, u32[]{:S(2)}, u32[]{:S(2)}) collective-permute-start(f32[1,128]{1,0:T(1,128)S(1)} %get-tuple-element.31), channel_id=1, source_target_pairs={{0,2},{2,4},{4,6},{6,0},{1,3},{3,5},{5,7},{7,1},{8,10},{10,12},{12... | collective-permute-start | bytes 1544 | tf_op jit(solution)/shard_map/ppermute | solution.py:265
  85.0 0.9 collective-permute-done.10
  86.0 1.3 %collective-permute-done.8 = f32[1,128]{1,0:T(1,128)S(1)} collective-permute-done((f32[1,128]{1,0:T(1,128)S(1)}, f32[1,128]{1,0:T(1,128)S(1)}, u32[]{:S(2)}, u32[]{:S(2)}) %collective-permute-start.8) | collective-permute-done | bytes 544 | tf_op jit(solution)/shard_map/ppermute | solution.py:265
  87.3 1.6 %collective-permute-done.9 = f32[1,128]{1,0:T(1,128)S(1)} collective-permute-done((f32[1,128]{1,0:T(1,128)S(1)}, f32[1,128]{1,0:T(1,128)S(1)}, u32[]{:S(2)}, u32[]{:S(2)}) %collective-permute-start.9) | collective-permute-done | bytes 544 | tf_op jit(solution)/shard_map/ppermute | solution.py:265
  88.9 0.6 broadcast_in_dim.6
  89.6 7.7 %all-to-all-start = ((f32[32,1,128]{2,1,0:T(1,128)}), f32[32,1,128]{2,1,0:T(1,128)S(1)}, u32[]{:S(2)}, u32[]{:S(2)}) async-start(f32[32,1,128]{2,1,0:T(1,128)} %broadcast_in_dim.6), calls=%async_computation | async-start | bytes 32768 | tf_op jit(solution)/shard_map/all_to_all | solution.py:217
  98.6 10.1 %all-to-all-done = f32[32,1,128]{2,1,0:T(1,128)S(1)} async-done(((f32[32,1,128]{2,1,0:T(1,128)}), f32[32,1,128]{2,1,0:T(1,128)S(1)}, u32[]{:S(2)}, u32[]{:S(2)}) %all-to-all-start) | async-done | bytes 16416 | tf_op jit(solution)/shard_map/all_to_all | solution.py:217
  108.9 0.7 multiply_add_fusion
  (29 shorter events, 1.7 us)
Async XLA Ops:
  0.6 42.2 %collective-permute-start = (bf16[256,2560]{1,0:T(8,128)(2,1)}, bf16[256,2560]{1,0:T(8,128)(2,1)S(1)}, u32[]{:S(2)}, u32[]{:S(2)}) collective-permute-start(bf16[256,2560]{1,0:T(8,128)(2,1)} %refs_0_.1), channel_id=1, source_target_pairs={{2,0},{127,1},{4,2},{1,3},{6,4},{3,5},{8,6},{5,7},{10,8},{7,9},{12... | collective-permute-start | bytes 3932168 | tf_op jit(solution)/shard_map/ppermute | solution.py:213
  2.9 47.0 %collective-permute-start.3 = (bf16[256,2560]{1,0:T(8,128)(2,1)}, bf16[256,2560]{1,0:T(8,128)(2,1)}, u32[]{:S(2)}, u32[]{:S(2)}) collective-permute-start(bf16[256,2560]{1,0:T(8,128)(2,1)} %refs_0_.1), channel_id=1, source_target_pairs={{0,1},{1,0},{2,3},{3,2},{4,5},{5,4},{6,7},{7,6},{8,9},{9,8},{10,11... | collective-permute-start | bytes 3932168 | tf_op jit(solution)/shard_map/ppermute | solution.py:213
  27.3 22.7 %copy-start = (bf16[256,2560]{1,0:T(8,128)(2,1)S(1)}, bf16[256,2560]{1,0:T(8,128)(2,1)}, u32[]{:S(2)}) copy-start(bf16[256,2560]{1,0:T(8,128)(2,1)} %queries.3) | copy-start | bytes 3932164
  28.8 1.3 %copy-start.1 = (bf16[256,2560]{1,0:T(8,128)(2,1)S(1)}, bf16[256,2560]{1,0:T(8,128)(2,1)}, u32[]{:S(2)}) copy-start(bf16[256,2560]{1,0:T(8,128)(2,1)} %values.1) | copy-start | bytes 3932164
  30.1 1.0 copy-start.3
  31.1 2.6 %copy-start.2 = (bf16[256,2560]{1,0:T(8,128)(2,1)S(1)}, bf16[256,2560]{1,0:T(8,128)(2,1)}, u32[]{:S(2)}) copy-start(bf16[256,2560]{1,0:T(8,128)(2,1)} %refs_0_.1) | copy-start | bytes 3932164
  33.6 16.4 %collective-permute-start.4 = (bf16[256,1280]{1,0:T(8,128)(2,1)S(1)}, bf16[256,1280]{1,0:T(8,128)(2,1)S(1)}, u32[]{:S(2)}, u32[]{:S(2)}) collective-permute-start(bf16[256,1280]{1,0:T(8,128)(2,1)S(1)} %shard_map.86.refs_2_), channel_id=1, source_target_pairs={{0,1},{1,0},{2,3},{3,2},{4,5},{5,4},{6,7},{7,6},{8,9},{9,8},{10,11... | collective-permute-start | bytes 1966088 | tf_op jit(solution)/shard_map/ppermute | solution.py:213
  33.7 30.9 %collective-permute-start.1 = (bf16[256,2560]{1,0:T(8,128)(2,1)S(1)}, bf16[256,2560]{1,0:T(8,128)(2,1)S(1)}, u32[]{:S(2)}, u32[]{:S(2)}) collective-permute-start(bf16[256,2560]{1,0:T(8,128)(2,1)S(1)} %copy-done.2), channel_id=1, source_target_pairs={{126,0},{3,1},{0,2},{5,3},{2,4},{7,5},{4,6},{9,7},{6,8},{11,9},{8,... | collective-permute-start | bytes 3932168 | tf_op jit(solution)/shard_map/ppermute | solution.py:213
  42.9 21.7 %collective-permute-start.2 = (bf16[256,2560]{1,0:T(8,128)(2,1)S(1)}, bf16[256,2560]{1,0:T(8,128)(2,1)S(1)}, u32[]{:S(2)}, u32[]{:S(2)}) collective-permute-start(bf16[256,2560]{1,0:T(8,128)(2,1)S(1)} %collective-permute-done.refs_0_), channel_id=1, source_target_pairs={{0,1},{1,0},{2,3},{3,2},{4,5},{5,4},{6,7},{7,6},{8,9},{9,8},{10,11... | collective-permute-start | bytes 3932168 | tf_op jit(solution)/shard_map/ppermute | solution.py:213
  58.9 15.3 %collective-permute-start.5 = (bf16[256,1280]{1,0:T(8,128)(2,1)S(1)}, bf16[256,1280]{1,0:T(8,128)(2,1)S(1)}, u32[]{:S(2)}, u32[]{:S(2)}) collective-permute-start(bf16[256,1280]{1,0:T(8,128)(2,1)S(1)} %shard_map.86.refs_2_), channel_id=1, source_target_pairs={{2,0},{127,1},{4,2},{1,3},{6,4},{3,5},{8,6},{5,7},{10,8},{7,9},{12... | collective-permute-start | bytes 1966088 | tf_op jit(solution)/shard_map/ppermute | solution.py:213
  59.0 22.0 %collective-permute-start.7 = (bf16[256,1280]{1,0:T(8,128)(2,1)S(1)}, bf16[256,1280]{1,0:T(8,128)(2,1)S(1)}, u32[]{:S(2)}, u32[]{:S(2)}) collective-permute-start(bf16[256,1280]{1,0:T(8,128)(2,1)S(1)} %shard_map.86.refs_2_), channel_id=1, source_target_pairs={{126,0},{3,1},{0,2},{5,3},{2,4},{7,5},{4,6},{9,7},{6,8},{11,9},{8,... | collective-permute-start | bytes 1966088 | tf_op jit(solution)/shard_map/ppermute | solution.py:213
  74.2 7.7 %collective-permute-start.6 = (bf16[256,1280]{1,0:T(8,128)(2,1)S(1)}, bf16[256,1280]{1,0:T(8,128)(2,1)S(1)}, u32[]{:S(2)}, u32[]{:S(2)}) collective-permute-start(bf16[256,1280]{1,0:T(8,128)(2,1)S(1)} %collective-permute-done.5.refs_1_), channel_id=1, source_target_pairs={{0,1},{1,0},{2,3},{3,2},{4,5},{5,4},{6,7},{7,6},{8,9},{9,8},{10,11... | collective-permute-start | bytes 1966088 | tf_op jit(solution)/shard_map/ppermute | solution.py:213
  81.9 15.4 %copy-start.4 = (s32[128]{0:T(128)S(1)}, s32[128]{0:T(128)}, u32[]{:S(2)}) copy-start(s32[128]{0:T(128)} %param.12) | copy-start | bytes 1540
  81.9 27.0 %copy-start.5 = (f32[64,256]{1,0:T(8,128)S(1)}, f32[64,256]{1,0:T(8,128)}, u32[]{:S(2)}) copy-start(f32[64,256]{1,0:T(8,128)} %param.11) | copy-start | bytes 196612
  83.5 2.5 %collective-permute-start.10 = (f32[1,128]{1,0:T(1,128)S(1)}, f32[1,128]{1,0:T(1,128)S(1)}, u32[]{:S(2)}, u32[]{:S(2)}) collective-permute-start(f32[1,128]{1,0:T(1,128)S(1)} %get-tuple-element.31), channel_id=1, source_target_pairs={{0,6},{2,0},{4,2},{6,4},{1,7},{3,1},{5,3},{7,5},{8,14},{10,8},{12,... | collective-permute-start | bytes 1544 | tf_op jit(solution)/shard_map/ppermute | solution.py:265
  83.6 3.7 %collective-permute-start.8 = (f32[1,128]{1,0:T(1,128)S(1)}, f32[1,128]{1,0:T(1,128)S(1)}, u32[]{:S(2)}, u32[]{:S(2)}) collective-permute-start(f32[1,128]{1,0:T(1,128)S(1)} %get-tuple-element.31), channel_id=1, source_target_pairs={{0,2},{2,4},{4,6},{6,0},{1,3},{3,5},{5,7},{7,1},{8,10},{10,12},{12... | collective-permute-start | bytes 1544 | tf_op jit(solution)/shard_map/ppermute | solution.py:265
  85.0 3.9 %collective-permute-start.9 = (f32[1,128]{1,0:T(1,128)S(1)}, f32[1,128]{1,0:T(1,128)S(1)}, u32[]{:S(2)}, u32[]{:S(2)}) collective-permute-start(f32[1,128]{1,0:T(1,128)S(1)} %get-tuple-element.31), channel_id=1, source_target_pairs={{0,4},{2,6},{4,0},{6,2},{1,5},{3,7},{5,1},{7,3},{8,12},{10,14},{12... | collective-permute-start | bytes 1544 | tf_op jit(solution)/shard_map/ppermute | solution.py:265
  89.6 19.2 %all-to-all-start = ((f32[32,1,128]{2,1,0:T(1,128)}), f32[32,1,128]{2,1,0:T(1,128)S(1)}, u32[]{:S(2)}, u32[]{:S(2)}) async-start(f32[32,1,128]{2,1,0:T(1,128)} %broadcast_in_dim.6), calls=%async_computation | async-start | bytes 32768 | tf_op jit(solution)/shard_map/all_to_all | solution.py:217

commit v3 on v2

--- a/solution.py
+++ b/solution.py
@@ -15,6 +15,7 @@
 LATENT_CH = 64
 PAIRS = HEADS // 2
 LANES = 2 * LATENT_CH
+OWN, _, NEAR, FAR, OVER = range(5)
 STEPS = 10
 Z_CORE = ("blk_0", "blk_2")
 BLK = ("blk_0", "blk_1", "blk_2")
@@ -107,56 +108,90 @@
     lax.fori_loop(0, PAIRS, one_pair, 0)
 
 
-def weights_kernel(counts, queries, *refs):
-    keys, (sums, tops, totals) = refs[:3], refs[3:6]
-    remote, own_sum = refs[6:9], refs[9]
+def merge_kernel(counts, queries, *refs):
+    keys, (sums, tops, totals) = refs[:2], refs[2:5]
+    near, over, new_sums, new_tops, new_totals = refs[5:]
     rows = queries.shape[0]
     columns = lax.broadcasted_iota(jnp.int32, (rows, LANES), 1)
-    block_counts = [counts[2 + block] for block in range(3)]
-    own_sum[...] = jnp.zeros_like(own_sum)
+    block_counts = [counts[NEAR], counts[OVER]]
 
     def one_pair(pair, carry):
-        scales = []
+        shrinks = []
         for side in range(2):
+            head = 2 * pair + side
             pieces = head_scores(queries, keys, pair, side, columns, block_counts)
-            own_top = tops[2 * pair + side]
+            own_top = tops[head]
             top = jnp.maximum(row_max(pieces), own_top)
             shrink = jnp.exp2(own_top - top)
             weights = [jnp.exp2(piece - top) for piece in pieces]
-            share = 1.0 / (row_sum(weights) + totals[2 * pair + side] * shrink)
-            per_block = len(weights) // len(remote)
+            new_tops[head] = top
+            new_totals[head] = row_sum(weights) + totals[head] * shrink
+            per_block = len(weights) // 2
             for at, weight in enumerate(weights):
                 block, half = divmod(at, per_block)
-                remote[block][2 * pair + side, :, half * LANES : (half + 1) * LANES] = (
-                    weight * share
-                ).astype(jnp.bfloat16)
-            scales.append(shrink * share)
-        scale = jnp.where(columns < LATENT_CH, *scales)
-        own_sum[...] += sums[:, columns_of(pair, LANES)] * scale
+                (near, over)[block][head, :, half * LANES : (half + 1) * LANES] = weight.astype(
+                    jnp.bfloat16
+                )
+            shrinks.append(shrink)
+        shrink = jnp.where(columns < LATENT_CH, *shrinks)
+        new_sums[:, columns_of(pair, LANES)] = sums[:, columns_of(pair, LANES)] * shrink
         return carry
 
     lax.fori_loop(0, PAIRS, one_pair, 0)
 
 
-def gather_kernel(blocks, finish, *refs):
-    shares, values = refs[:blocks], refs[blocks : 2 * blocks]
-    start = refs[2 * blocks]
-    even_sum = jnp.zeros(start.shape, jnp.float32)
-    odd_sum = jnp.zeros(start.shape, jnp.float32)
+def collect_kernel(near, over, near_values, over_values, sums, scales, out):
+    low = lax.broadcasted_iota(jnp.int32, out.shape, 1) < LATENT_CH
+    total = jnp.zeros(out.shape, jnp.float32)
     for pair in range(PAIRS):
-        for block in range(blocks):
-            value = values[block][:, pair * LANES : (pair + 1) * LANES]
-            even_sum += dot_plain(shares[block][2 * pair], value)
-            odd_sum += dot_plain(shares[block][2 * pair + 1], value)
-    low = lax.broadcasted_iota(jnp.int32, start.shape, 1) < LATENT_CH
-    both = start[...] + jnp.where(low, even_sum, odd_sum)
-    if not finish:
-        refs[-1][...] = both
-        return
-    counts, out, squares = refs[-3:]
+        lanes = slice(pair * LANES, (pair + 1) * LANES)
+        even, odd = [
+            dot_plain(near[head], near_values[:, lanes])
+            + dot_plain(over[head], over_values[:, lanes])
+            for head in (2 * pair, 2 * pair + 1)
+        ]
+        total += (sums[:, lanes] + jnp.where(low, even, odd)) * scales[pair]
+    out[...] = total
+
+
+def weights_kernel(counts, queries, keys, tops, totals, shares, scales):
+    rows = queries.shape[0]
+    columns = lax.broadcasted_iota(jnp.int32, (rows, LANES), 1)
+    block_counts = [counts[FAR]]
+
+    def one_pair(pair, carry):
+        factors = []
+        for side in range(2):
+            head = 2 * pair + side
+            pieces = head_scores(queries, [keys], pair, side, columns, block_counts)
+            old_top = tops[head]
+            top = jnp.maximum(row_max(pieces), old_top)
+            shrink = jnp.exp2(old_top - top)
+            weights = [jnp.exp2(piece - top) for piece in pieces]
+            share = 1.0 / (row_sum(weights) + totals[head] * shrink)
+            for half, weight in enumerate(weights):
+                shares[head, :, half * LANES : (half + 1) * LANES] = (weight * share).astype(
+                    jnp.bfloat16
+                )
+            factors.append(shrink * share)
+        scales[pair] = jnp.where(columns < LATENT_CH, *factors)
+        return carry
+
+    lax.fori_loop(0, PAIRS, one_pair, 0)
+
+
+def finish_kernel(shares, values, most, counts, out, squares):
+    even_sum = jnp.zeros(most.shape, jnp.float32)
+    odd_sum = jnp.zeros(most.shape, jnp.float32)
+    for pair in range(PAIRS):
+        value = values[:, pair * LANES : (pair + 1) * LANES]
+        even_sum += dot_plain(shares[2 * pair], value)
+        odd_sum += dot_plain(shares[2 * pair + 1], value)
+    low = lax.broadcasted_iota(jnp.int32, most.shape, 1) < LATENT_CH
+    both = most[...] + jnp.where(low, even_sum, odd_sum)
     both = both + pltpu.roll(both, LATENT_CH, 1)
     vel = jnp.transpose(both)[:LATENT_CH]
-    used = lax.broadcasted_iota(jnp.int32, vel.shape, 1) < counts[0]
+    used = lax.broadcasted_iota(jnp.int32, vel.shape, 1) < counts[OWN]
     vel = jnp.where(used, vel, 0.0)
     out[...] = vel
     square = jnp.sum(vel * vel, axis=0, keepdims=True)
@@ -191,22 +226,27 @@
     return call(own_kernel, 0, (counts, queries, *keys, *projected), outs)
 
 
-def attention_weights(counts, queries, keys, own):
-    rows = queries.shape[0]
-    outs = [((HEADS, rows, rows), jnp.bfloat16)] * 3 + [((rows, LANES), jnp.float32)]
-    return call(weights_kernel, 0, (counts, queries, *keys, *own), outs)
-
-
-def gather(shares, values, start, counts=None, copies=1):
-    rows = start.shape[0]
-    blocks = len(shares)
-    operands = [*shares, *values, start]
-    if counts is None:
-        kernel = functools.partial(gather_kernel, blocks, False)
-        return call(kernel, -1, operands, [((rows, LANES), jnp.float32)])[0]
-    kernel = functools.partial(gather_kernel, blocks, True)
-    outs = [((LATENT_CH, rows), jnp.float32), ((copies, LANES), jnp.float32)]
-    return call(kernel, len(operands), [*operands, counts], outs)
+def merge(counts, queries, keys, own):
+    rows = queries.shape[0]
+    outs = [((HEADS, rows, rows), jnp.bfloat16)] * 2 + [((rows, PAIRS * LANES), jnp.float32)]
+    outs += [((HEADS, rows, LANES), jnp.float32)] * 2
+    return call(merge_kernel, 0, (counts, queries, *keys, *own), outs)
+
+
+def collect(weights, values, sums, scales):
+    outs = [((sums.shape[0], LANES), jnp.float32)]
+    return call(collect_kernel, -1, (*weights, *values, sums, scales), outs)[0]
+
+
+def last_weights(counts, queries, keys, tops, totals):
+    rows = queries.shape[0]
+    outs = [((HEADS, rows, rows), jnp.bfloat16), ((PAIRS, rows, LANES), jnp.float32)]
+    return call(weights_kernel, 0, (counts, queries, keys, tops, totals), outs)
+
+
+def finish(shares, values, most, counts):
+    outs = [((LATENT_CH, most.shape[0]), jnp.float32), ((1, LANES), jnp.float32)]
+    return call(finish_kernel, 3, (shares, values, most, counts), outs)
 
 
 def exchange(shard, pairs):
@@ -237,28 +277,24 @@
     keys_far = exchange(keys, far_pairs)
     keys_partner = exchange(keys, chip_pairs)
     projected = project(counts, values, out_weight)
+    projected_near = exchange(projected, near_pairs)
     projected_partner = exchange(projected, chip_pairs)
-    own = own_attention(
+    own_sums, own_tops, own_totals = own_attention(
         counts, queries, (keys, keys_partner), (projected, projected_partner)
     )
-    projected, *own = lax.optimization_barrier((projected, *own))
-    projected_near = exchange(projected, near_pairs)
+    projected, own_sums = lax.optimization_barrier((projected, own_sums))
     projected_far = exchange(projected, far_pairs)
     keys_over = exchange(keys_near, chip_pairs)
-    shares_near, shares_far, shares_over, own_sum = attention_weights(
-        counts, queries, (keys_near, keys_far, keys_over), own
-    )
-    projected_near, own_sum = lax.optimization_barrier((projected_near, own_sum))
+    weights_near, weights_over, sums, tops, totals = merge(
+        counts, queries, (keys_near, keys_over), (own_sums, own_tops, own_totals)
+    )
+    projected_near, sums = lax.optimization_barrier((projected_near, sums))
     projected_over = exchange(projected_near, chip_pairs)
-    most = gather((shares_near,), (projected_near,), own_sum)
-    most = gather((shares_far,), (projected_far,), most)
-    vel, squares = gather(
-        (shares_over,),
-        (projected_over,),
-        most,
-        counts,
-        1,
-    )
+    shares, scales = last_weights(counts, queries, keys_far, tops, totals)
+    most = collect(
+        (weights_near, weights_over), (projected_near, projected_over), sums, scales
+    )
+    vel, squares = finish(shares, projected_far, most, counts)
 
     columns = lax.axis_size("blk_1")
     moved = [

time: 110 us -> 111 us (level)
  starting transfers between devices: 54.4 us -> 47.5 us
  waiting for transfers between devices: 23.7 us -> 29.1 us
  Pallas kernels: 23.4 us -> 26.2 us
    ppermute x8, starting transfers between devices: 45.2 us -> 39.1 us  [exchange(): return lax.ppermute(shard, BLK, pairs)]
    ppermute x8, waiting for transfers between devices: 9.62 us -> 14.7 us  [exchange(): return lax.ppermute(shard, BLK, pairs)]
    pallas_call x6, Pallas kernels: 23.4 us -> 26.2 us  [call(): pl.pallas_call(kernel, in_specs=[scalars if at == counts_first else here...]
  transfers between devices with their start and end apart: 12 -> 12, of which waited for: 6 -> 6; matrix products, arithmetic and copies ran while one was open for 2% -> 2% of each run, Pallas kernels for 20% -> 22%
where the time goes in v3:
time: 111 us
  starting transfers between devices  47.5 us (43%)
  waiting for transfers between devices  29.1 us (26%)
  Pallas kernels  26.2 us (24%)
  local copies, waits for them, and re-layouts  4.51 us (4%)
  between operations  2.27 us (2%)
  other arithmetic  1.32 us (1%)
    ppermute x8, starting transfers between devices, exchange(): return lax.ppermute(shard, BLK, pairs)  39.1 us
    pallas_call x6, Pallas kernels, call(): pl.pallas_call(kernel, in_specs=[scalars if at == counts_first else here...  26.2 us
    ppermute x8, waiting for transfers between devices, exchange(): return lax.ppermute(shard, BLK, pairs)  14.7 us
    all_to_all x1, waiting for transfers between devices, exchanged_sum(): gathered = lax.all_to_all(copies, axes, 0, 0, tiled=True)  10.5 us
    all_to_all x1, starting transfers between devices, exchanged_sum(): gathered = lax.all_to_all(copies, axes, 0, 0, tiled=True)  6.89 us
    ppermute x3, waiting for transfers between devices, step(): lax.ppermute(squares, 'blk_1', [(i, (i + by) % columns) for i in range(co...  3.92 us
    unnamed x12, local copies, waits for them, and re-layouts  2.31 us
  transfers between devices with their start and end apart: 12, of which 6 were waited for; matrix products, arithmetic and copies ran while one was open for 2% of the time, Pallas kernels for 22%

profile of v3, /device:TPU:33, one launch (start us, length us, event | category | flops | bytes accessed | tf_op | source)
XLA Modules:
  0.0 110.9 jit_solution(633957548313545909)
XLA Ops:
  0.6 2.3 %collective-permute-start.1 = (bf16[256,2560]{1,0:T(8,128)(2,1)}, bf16[256,2560]{1,0:T(8,128)(2,1)}, u32[]{:S(2)}, u32[]{:S(2)}) collective-permute-start(bf16[256,2560]{1,0:T(8,128)(2,1)} %refs_0_.1), channel_id=1, source_target_pairs={{2,0},{127,1},{4,2},{1,3},{6,4},{3,5},{8,6},{5,7},{10,8},{7,9},{12... | collective-permute-start | bytes 3932168 | tf_op jit(solution)/shard_map/ppermute | solution.py:253
  2.9 24.2 %collective-permute-start.3 = (bf16[256,2560]{1,0:T(8,128)(2,1)}, bf16[256,2560]{1,0:T(8,128)(2,1)S(1)}, u32[]{:S(2)}, u32[]{:S(2)}) collective-permute-start(bf16[256,2560]{1,0:T(8,128)(2,1)} %refs_0_.1), channel_id=1, source_target_pairs={{0,1},{1,0},{2,3},{3,2},{4,5},{5,4},{6,7},{7,6},{8,9},{9,8},{10,11... | collective-permute-start | bytes 3932168 | tf_op jit(solution)/shard_map/ppermute | solution.py:253
  27.1 14.4 %collective-permute-done.1.refs_0_ = bf16[256,2560]{1,0:T(8,128)(2,1)} collective-permute-done((bf16[256,2560]{1,0:T(8,128)(2,1)}, bf16[256,2560]{1,0:T(8,128)(2,1)}, u32[]{:S(2)}, u32[]{:S(2)}) %collective-permute-start.1) | collective-permute-done | bytes 1310752 | tf_op jit(solution)/shard_map/ppermute | solution.py:253
  41.6 1.0 collective-permute-start.2
  42.7 1.4 %gather_fusion = s32[5]{0:T(128)S(1)} fusion(s32[128]{0:T(128)} %param.12, s32[1024]{0:T(1024)S(1)} %pad_clamp_fusion), kind=kCustom, calls=%fused_computation | custom fusion | bytes 60 | tf_op jit(solution)/shard_map/gather | solution.py:274
  44.2 1.3 %copy-done.1 = bf16[256,2560]{1,0:T(8,128)(2,1)S(1)} copy-done((bf16[256,2560]{1,0:T(8,128)(2,1)S(1)}, bf16[256,2560]{1,0:T(8,128)(2,1)}, u32[]{:S(2)}) %copy-start.1) | copy-done | bytes 1310744
  45.5 1.0 copy-done.3
  46.5 2.5 %shard_map.86.refs_2_ = bf16[256,1280]{1,0:T(8,128)(2,1)S(1)} custom-call(s32[5]{0:T(128)S(1)} %and_select_fusion.counts, bf16[256,2560]{1,0:T(8,128)(2,1)S(1)} %copy-done.1, bf16[64,2560]{1,0:T(8,128)(2,1)S(1)} %copy-done.3), custom_call_target="tpu_custom_call" | custom-call | tf_op jit(solution)/shard_map/pallas_call | solution.py:208
  49.3 5.6 %collective-permute-start = (bf16[256,2560]{1,0:T(8,128)(2,1)S(1)}, bf16[256,2560]{1,0:T(8,128)(2,1)S(1)}, u32[]{:S(2)}, u32[]{:S(2)}) collective-permute-start(bf16[256,2560]{1,0:T(8,128)(2,1)S(1)} %copy-done.2), channel_id=1, source_target_pairs={{126,0},{3,1},{0,2},{5,3},{2,4},{7,5},{4,6},{9,7},{6,8},{11,9},{8,... | collective-permute-start | bytes 3932168 | tf_op jit(solution)/shard_map/ppermute | solution.py:253
  54.9 8.2 %shard_map.87 = (f32[256,1280]{1,0:T(8,128)S(1)}, f32[20,256,128]{2,1,0:T(8,128)S(1)}, f32[20,256,128]{2,1,0:T(8,128)S(1)}) custom-call(s32[5]{0:T(128)S(1)} %and_select_fusion.counts, bf16[256,2560]{1,0:T(8,128)(2,1)S(1)} %copy-done, bf16[256,2560]{1,0:T(8,128)(2,1)S(1)} %copy-done.2, bf16[256,2560]{1,0:T(8,128)(2,1)S(1)} %collective-permute-done.3.refs_1_, ...), custom_call_target="tpu_custom_call" | custom-call | tf_op jit(solution)/shard_map/pallas_call | solution.py:208
  63.1 7.4 %shard_map.88 = (bf16[20,256,256]{2,1,0:T(8,128)(2,1)S(1)}, bf16[20,256,256]{2,1,0:T(8,128)(2,1)S(1)}, f32[256,1280]{1,0:T(8,128)S(1)}, f32[20,256,128]{2,1,0:T(8,128)S(1)}, f32[20,256,128]{2,1,0:T(8,128)S(1)}) custom-call(s32[5]{0:T(128)S(1)} %and_select_fusion.counts, bf16[256,2560]{1,0:T(8,128)(2,1)S(1)} %copy-done, ...), custom_call_target="tpu_custom_call" | custom-call | tf_op jit(solution)/shard_map/pallas_call | solution.py:208
  70.5 0.6 collective-permute-start.7
  71.1 5.0 %collective-permute-start.5 = (bf16[256,1280]{1,0:T(8,128)(2,1)S(1)}, bf16[256,1280]{1,0:T(8,128)(2,1)S(1)}, u32[]{:S(2)}, u32[]{:S(2)}) collective-permute-start(bf16[256,1280]{1,0:T(8,128)(2,1)S(1)} %shard_map.86.refs_2_), channel_id=1, source_target_pairs={{126,0},{3,1},{0,2},{5,3},{2,4},{7,5},{4,6},{9,7},{6,8},{11,9},{8,... | collective-permute-start | bytes 1966088 | tf_op jit(solution)/shard_map/ppermute | solution.py:253
  76.9 5.1 %shard_map.89 = (bf16[20,256,256]{2,1,0:T(8,128)(2,1)S(1)}, f32[10,256,128]{2,1,0:T(8,128)S(1)}) custom-call(s32[5]{0:T(128)S(1)} %and_select_fusion.counts, bf16[256,2560]{1,0:T(8,128)(2,1)S(1)} %copy-done, bf16[256,2560]{1,0:T(8,128)(2,1)S(1)} %collective-permute-done.keys, f32[20,256,128]{2,1,0:T(8,128)S(1)} %get-tuple-element.22.tops, ...), custom_call_target="tpu_custom_call" | custom-call | tf_op jit(solution)/shard_map/pallas_call | solution.py:208
  81.9 1.6 %shard_map.90.most = f32[256,128]{1,0:T(8,128)S(1)} custom-call(bf16[20,256,256]{2,1,0:T(8,128)(2,1)S(1)} %get-tuple-element.26.near, bf16[20,256,256]{2,1,0:T(8,128)(2,1)S(1)} %get-tuple-element.27.over, bf16[256,1280]{1,0:T(8,128)(2,1)S(1)} %collective-permute-done.6.near_values, bf16[256,1280]{1,0:T(8,128)(2,1)S(1)} %collective-permute-done.7.over_values, ...), custom_call_target="tpu_custom_call" | custom-call | tf_op jit(solution)/shard_map/pallas_call | solution.py:208
  83.7 1.6 %shard_map.91 = (f32[64,256]{1,0:T(8,128)S(1)}, f32[1,128]{1,0:T(1,128)S(1)}) custom-call(bf16[20,256,256]{2,1,0:T(8,128)(2,1)S(1)} %get-tuple-element.24.shares, bf16[256,1280]{1,0:T(8,128)(2,1)S(1)} %collective-permute-done.5.values, f32[256,128]{1,0:T(8,128)S(1)} %shard_map.90.most, s32[5]{0:T(128)S(1)} %and_select_fusion.counts), custom_call_target="tpu_custom_call" | custom-call | tf_op jit(solution)/shard_map/pallas_call | solution.py:208
  85.4 1.4 %collective-permute-start.8 = (f32[1,128]{1,0:T(1,128)S(1)}, f32[1,128]{1,0:T(1,128)S(1)}, u32[]{:S(2)}, u32[]{:S(2)}) collective-permute-start(f32[1,128]{1,0:T(1,128)S(1)} %get-tuple-element.33), channel_id=1, source_target_pairs={{0,2},{2,4},{4,6},{6,0},{1,3},{3,5},{5,7},{7,1},{8,10},{10,12},{12... | collective-permute-start | bytes 1544 | tf_op jit(solution)/shard_map/ppermute | solution.py:301
  86.8 0.9 collective-permute-done.10
  87.8 1.3 %collective-permute-done.8 = f32[1,128]{1,0:T(1,128)S(1)} collective-permute-done((f32[1,128]{1,0:T(1,128)S(1)}, f32[1,128]{1,0:T(1,128)S(1)}, u32[]{:S(2)}, u32[]{:S(2)}) %collective-permute-start.8) | collective-permute-done | bytes 544 | tf_op jit(solution)/shard_map/ppermute | solution.py:301
  89.1 1.6 %collective-permute-done.9 = f32[1,128]{1,0:T(1,128)S(1)} collective-permute-done((f32[1,128]{1,0:T(1,128)S(1)}, f32[1,128]{1,0:T(1,128)S(1)}, u32[]{:S(2)}, u32[]{:S(2)}) %collective-permute-start.9) | collective-permute-done | bytes 544 | tf_op jit(solution)/shard_map/ppermute | solution.py:301
  90.7 0.6 broadcast_in_dim.6
  91.4 6.9 %all-to-all-start = ((f32[32,1,128]{2,1,0:T(1,128)}), f32[32,1,128]{2,1,0:T(1,128)S(1)}, u32[]{:S(2)}, u32[]{:S(2)}) async-start(f32[32,1,128]{2,1,0:T(1,128)} %broadcast_in_dim.6), calls=%async_computation | async-start | bytes 32768 | tf_op jit(solution)/shard_map/all_to_all | solution.py:257
  99.6 10.5 %all-to-all-done = f32[32,1,128]{2,1,0:T(1,128)S(1)} async-done(((f32[32,1,128]{2,1,0:T(1,128)}), f32[32,1,128]{2,1,0:T(1,128)S(1)}, u32[]{:S(2)}, u32[]{:S(2)}) %all-to-all-start) | async-done | bytes 16416 | tf_op jit(solution)/shard_map/all_to_all | solution.py:257
  110.2 0.7 multiply_add_fusion
  (29 shorter events, 1.4 us)
Async XLA Ops:
  0.6 41.0 %collective-permute-start.1 = (bf16[256,2560]{1,0:T(8,128)(2,1)}, bf16[256,2560]{1,0:T(8,128)(2,1)}, u32[]{:S(2)}, u32[]{:S(2)}) collective-permute-start(bf16[256,2560]{1,0:T(8,128)(2,1)} %refs_0_.1), channel_id=1, source_target_pairs={{2,0},{127,1},{4,2},{1,3},{6,4},{3,5},{8,6},{5,7},{10,8},{7,9},{12... | collective-permute-start | bytes 3932168 | tf_op jit(solution)/shard_map/ppermute | solution.py:253
  2.9 52.0 %collective-permute-start.3 = (bf16[256,2560]{1,0:T(8,128)(2,1)}, bf16[256,2560]{1,0:T(8,128)(2,1)S(1)}, u32[]{:S(2)}, u32[]{:S(2)}) collective-permute-start(bf16[256,2560]{1,0:T(8,128)(2,1)} %refs_0_.1), channel_id=1, source_target_pairs={{0,1},{1,0},{2,3},{3,2},{4,5},{5,4},{6,7},{7,6},{8,9},{9,8},{10,11... | collective-permute-start | bytes 3932168 | tf_op jit(solution)/shard_map/ppermute | solution.py:253
  41.6 21.5 %collective-permute-start.2 = (bf16[256,2560]{1,0:T(8,128)(2,1)}, bf16[256,2560]{1,0:T(8,128)(2,1)}, u32[]{:S(2)}, u32[]{:S(2)}) collective-permute-start(bf16[256,2560]{1,0:T(8,128)(2,1)} %collective-permute-done.1.refs_0_), channel_id=1, source_target_pairs={{0,1},{1,0},{2,3},{3,2},{4,5},{5,4},{6,7},{7,6},{8,9},{9,8},{10,11... | collective-permute-start | bytes 3932168 | tf_op jit(solution)/shard_map/ppermute | solution.py:253
  42.7 12.2 %copy-start = (bf16[256,2560]{1,0:T(8,128)(2,1)S(1)}, bf16[256,2560]{1,0:T(8,128)(2,1)}, u32[]{:S(2)}) copy-start(bf16[256,2560]{1,0:T(8,128)(2,1)} %queries.5) | copy-start | bytes 3932164
  44.2 1.3 %copy-start.1 = (bf16[256,2560]{1,0:T(8,128)(2,1)S(1)}, bf16[256,2560]{1,0:T(8,128)(2,1)}, u32[]{:S(2)}) copy-start(bf16[256,2560]{1,0:T(8,128)(2,1)} %values.1) | copy-start | bytes 3932164
  45.5 1.0 copy-start.3
  46.5 2.8 %copy-start.2 = (bf16[256,2560]{1,0:T(8,128)(2,1)S(1)}, bf16[256,2560]{1,0:T(8,128)(2,1)}, u32[]{:S(2)}) copy-start(bf16[256,2560]{1,0:T(8,128)(2,1)} %refs_0_.1) | copy-start | bytes 3932164
  49.0 5.9 %collective-permute-start.4 = (bf16[256,1280]{1,0:T(8,128)(2,1)S(1)}, bf16[256,1280]{1,0:T(8,128)(2,1)S(1)}, u32[]{:S(2)}, u32[]{:S(2)}) collective-permute-start(bf16[256,1280]{1,0:T(8,128)(2,1)S(1)} %shard_map.86.refs_2_), channel_id=1, source_target_pairs={{0,1},{1,0},{2,3},{3,2},{4,5},{5,4},{6,7},{7,6},{8,9},{9,8},{10,11... | collective-permute-start | bytes 1966088 | tf_op jit(solution)/shard_map/ppermute | solution.py:253
  49.1 21.3 %collective-permute-start.6 = (bf16[256,1280]{1,0:T(8,128)(2,1)S(1)}, bf16[256,1280]{1,0:T(8,128)(2,1)S(1)}, u32[]{:S(2)}, u32[]{:S(2)}) collective-permute-start(bf16[256,1280]{1,0:T(8,128)(2,1)S(1)} %shard_map.86.refs_2_), channel_id=1, source_target_pairs={{2,0},{127,1},{4,2},{1,3},{6,4},{3,5},{8,6},{5,7},{10,8},{7,9},{12... | collective-permute-start | bytes 1966088 | tf_op jit(solution)/shard_map/ppermute | solution.py:253
  49.3 27.6 %collective-permute-start = (bf16[256,2560]{1,0:T(8,128)(2,1)S(1)}, bf16[256,2560]{1,0:T(8,128)(2,1)S(1)}, u32[]{:S(2)}, u32[]{:S(2)}) collective-permute-start(bf16[256,2560]{1,0:T(8,128)(2,1)S(1)} %copy-done.2), channel_id=1, source_target_pairs={{126,0},{3,1},{0,2},{5,3},{2,4},{7,5},{4,6},{9,7},{6,8},{11,9},{8,... | collective-permute-start | bytes 3932168 | tf_op jit(solution)/shard_map/ppermute | solution.py:253
  70.5 11.4 %collective-permute-start.7 = (bf16[256,1280]{1,0:T(8,128)(2,1)S(1)}, bf16[256,1280]{1,0:T(8,128)(2,1)S(1)}, u32[]{:S(2)}, u32[]{:S(2)}) collective-permute-start(bf16[256,1280]{1,0:T(8,128)(2,1)S(1)} %collective-permute-done.6.near_values), channel_id=1, source_target_pairs={{0,1},{1,0},{2,3},{3,2},{4,5},{5,4},{6,7},{7,6},{8,9},{9,8},{10,11... | collective-permute-start | bytes 1966088 | tf_op jit(solution)/shard_map/ppermute | solution.py:253
  71.1 12.6 %collective-permute-start.5 = (bf16[256,1280]{1,0:T(8,128)(2,1)S(1)}, bf16[256,1280]{1,0:T(8,128)(2,1)S(1)}, u32[]{:S(2)}, u32[]{:S(2)}) collective-permute-start(bf16[256,1280]{1,0:T(8,128)(2,1)S(1)} %shard_map.86.refs_2_), channel_id=1, source_target_pairs={{126,0},{3,1},{0,2},{5,3},{2,4},{7,5},{4,6},{9,7},{6,8},{11,9},{8,... | collective-permute-start | bytes 1966088 | tf_op jit(solution)/shard_map/ppermute | solution.py:253
  83.7 14.5 %copy-start.4 = (s32[128]{0:T(128)S(1)}, s32[128]{0:T(128)}, u32[]{:S(2)}) copy-start(s32[128]{0:T(128)} %param.12) | copy-start | bytes 1540
  83.7 26.5 %copy-start.5 = (f32[64,256]{1,0:T(8,128)S(1)}, f32[64,256]{1,0:T(8,128)}, u32[]{:S(2)}) copy-start(f32[64,256]{1,0:T(8,128)} %param.11) | copy-start | bytes 196612
  85.3 2.5 %collective-permute-start.10 = (f32[1,128]{1,0:T(1,128)S(1)}, f32[1,128]{1,0:T(1,128)S(1)}, u32[]{:S(2)}, u32[]{:S(2)}) collective-permute-start(f32[1,128]{1,0:T(1,128)S(1)} %get-tuple-element.33), channel_id=1, source_target_pairs={{0,6},{2,0},{4,2},{6,4},{1,7},{3,1},{5,3},{7,5},{8,14},{10,8},{12,... | collective-permute-start | bytes 1544 | tf_op jit(solution)/shard_map/ppermute | solution.py:301
  85.4 3.7 %collective-permute-start.8 = (f32[1,128]{1,0:T(1,128)S(1)}, f32[1,128]{1,0:T(1,128)S(1)}, u32[]{:S(2)}, u32[]{:S(2)}) collective-permute-start(f32[1,128]{1,0:T(1,128)S(1)} %get-tuple-element.33), channel_id=1, source_target_pairs={{0,2},{2,4},{4,6},{6,0},{1,3},{3,5},{5,7},{7,1},{8,10},{10,12},{12... | collective-permute-start | bytes 1544 | tf_op jit(solution)/shard_map/ppermute | solution.py:301
  86.8 3.9 %collective-permute-start.9 = (f32[1,128]{1,0:T(1,128)S(1)}, f32[1,128]{1,0:T(1,128)S(1)}, u32[]{:S(2)}, u32[]{:S(2)}) collective-permute-start(f32[1,128]{1,0:T(1,128)S(1)} %get-tuple-element.33), channel_id=1, source_target_pairs={{0,4},{2,6},{4,0},{6,2},{1,5},{3,7},{5,1},{7,3},{8,12},{10,14},{12... | collective-permute-start | bytes 1544 | tf_op jit(solution)/shard_map/ppermute | solution.py:301
  91.4 18.7 %all-to-all-start = ((f32[32,1,128]{2,1,0:T(1,128)}), f32[32,1,128]{2,1,0:T(1,128)S(1)}, u32[]{:S(2)}, u32[]{:S(2)}) async-start(f32[32,1,128]{2,1,0:T(1,128)} %broadcast_in_dim.6), calls=%async_computation | async-start | bytes 32768 | tf_op jit(solution)/shard_map/all_to_all | solution.py:257

commit v4 on v3

--- a/solution.py
+++ b/solution.py
@@ -15,7 +15,7 @@
 LATENT_CH = 64
 PAIRS = HEADS // 2
 LANES = 2 * LATENT_CH
-OWN, _, NEAR, FAR, OVER = range(5)
+OWN, PARTNER, NEAR, FAR, OVER = range(5)
 STEPS = 10
 Z_CORE = ("blk_0", "blk_2")
 BLK = ("blk_0", "blk_1", "blk_2")
@@ -41,8 +41,9 @@
 def project_kernel(counts, values, weight, out):
     def one_pair(pair, carry):
         held = values[:, columns_of(pair, 2 * HEAD_DIM)]
-        used = lax.broadcasted_iota(jnp.int32, held.shape, 0) < counts[0]
-        held = jnp.where(used, held, jnp.zeros_like(held))
+        used = lax.broadcasted_iota(jnp.int32, (held.shape[0], LANES), 0) < counts[OWN : OWN + 1, :]
+        halves = [held[:, :LANES], held[:, LANES:]]
+        held = jnp.concatenate([jnp.where(used, x, jnp.zeros_like(x)) for x in halves], axis=1)
         part = weight[:, columns_of(pair, 2 * HEAD_DIM)]
         even = lax.broadcasted_iota(jnp.int32, part.shape, 1) < HEAD_DIM
         zero = jnp.zeros_like(part)
@@ -82,7 +83,7 @@
     sums, tops, totals = refs[4:]
     rows = queries.shape[0]
     columns = lax.broadcasted_iota(jnp.int32, (rows, LANES), 1)
-    block_counts = [counts[block] for block in range(2)]
+    block_counts = [counts[block : block + 1, :] for block in (OWN, PARTNER)]
 
     def one_pair(pair, carry):
         parts = []
@@ -113,7 +114,7 @@
     near, over, new_sums, new_tops, new_totals = refs[5:]
     rows = queries.shape[0]
     columns = lax.broadcasted_iota(jnp.int32, (rows, LANES), 1)
-    block_counts = [counts[NEAR], counts[OVER]]
+    block_counts = [counts[block : block + 1, :] for block in (NEAR, OVER)]
 
     def one_pair(pair, carry):
         shrinks = []
@@ -145,9 +146,9 @@
     total = jnp.zeros(out.shape, jnp.float32)
     for pair in range(PAIRS):
         lanes = slice(pair * LANES, (pair + 1) * LANES)
+        stacked = jnp.concatenate([near_values[:, lanes], over_values[:, lanes]], axis=0)
         even, odd = [
-            dot_plain(near[head], near_values[:, lanes])
-            + dot_plain(over[head], over_values[:, lanes])
+            dot_plain(jnp.concatenate([near[head], over[head]], axis=1), stacked)
             for head in (2 * pair, 2 * pair + 1)
         ]
         total += (sums[:, lanes] + jnp.where(low, even, odd)) * scales[pair]
@@ -157,7 +158,7 @@
 def weights_kernel(counts, queries, keys, tops, totals, shares, scales):
     rows = queries.shape[0]
     columns = lax.broadcasted_iota(jnp.int32, (rows, LANES), 1)
-    block_counts = [counts[FAR]]
+    block_counts = [counts[FAR : FAR + 1, :]]
 
     def one_pair(pair, carry):
         factors = []
@@ -181,72 +182,67 @@
 
 
 def finish_kernel(shares, values, most, counts, out, squares):
-    even_sum = jnp.zeros(most.shape, jnp.float32)
-    odd_sum = jnp.zeros(most.shape, jnp.float32)
-    for pair in range(PAIRS):
-        value = values[:, pair * LANES : (pair + 1) * LANES]
-        even_sum += dot_plain(shares[2 * pair], value)
-        odd_sum += dot_plain(shares[2 * pair + 1], value)
+    stacked = jnp.concatenate(
+        [values[:, pair * LANES : (pair + 1) * LANES] for pair in range(PAIRS)], axis=0
+    )
+    even_sum, odd_sum = [
+        dot_plain(jnp.concatenate([shares[2 * pair + side] for pair in range(PAIRS)], axis=1), stacked)
+        for side in range(2)
+    ]
     low = lax.broadcasted_iota(jnp.int32, most.shape, 1) < LATENT_CH
     both = most[...] + jnp.where(low, even_sum, odd_sum)
     both = both + pltpu.roll(both, LATENT_CH, 1)
-    vel = jnp.transpose(both)[:LATENT_CH]
-    used = lax.broadcasted_iota(jnp.int32, vel.shape, 1) < counts[OWN]
-    vel = jnp.where(used, vel, 0.0)
+    used = lax.broadcasted_iota(jnp.int32, both.shape, 0) < counts[OWN : OWN + 1, :]
+    vel = jnp.transpose(jnp.where(used, both, 0.0))[:LATENT_CH]
     out[...] = vel
     square = jnp.sum(vel * vel, axis=0, keepdims=True)
     squares[...] = jnp.broadcast_to(jnp.sum(square, axis=1, keepdims=True), squares.shape)
 
 
-def call(kernel, counts_first, operands, outs, limit=24):
+def call(kernel, operands, outs):
     here = pl.BlockSpec(memory_space=pltpu.VMEM)
-    scalars = pl.BlockSpec(memory_space=pltpu.SMEM)
-    operands = [
-        x if at == counts_first else pltpu.with_memory_space_constraint(x, pltpu.VMEM)
-        for at, x in enumerate(operands)
-    ]
     return pl.pallas_call(
         kernel,
-        in_specs=[scalars if at == counts_first else here for at in range(len(operands))],
+        in_specs=[here] * len(operands),
         out_specs=[here] * len(outs),
         out_shape=[pltpu.VMEM(shape, dtype) for shape, dtype in outs],
-        compiler_params=pltpu.CompilerParams(vmem_limit_bytes=limit << 20),
-    )(*operands)
+        compiler_params=pltpu.CompilerParams(vmem_limit_bytes=24 << 20),
+    )(*[pltpu.with_memory_space_constraint(x, pltpu.VMEM) for x in operands])
 
 
 def project(counts, values, weight):
     rows = values.shape[0]
     outs = [((rows, PAIRS * LANES), jnp.bfloat16)]
-    return call(project_kernel, 0, (counts, values, weight), outs)[0]
+    return call(project_kernel, (counts, values, weight), outs)[0]
 
 
 def own_attention(counts, queries, keys, projected):
     rows = queries.shape[0]
     outs = [((rows, PAIRS * LANES), jnp.float32)] + [((HEADS, rows, LANES), jnp.float32)] * 2
-    return call(own_kernel, 0, (counts, queries, *keys, *projected), outs)
+    return call(own_kernel, (counts, queries, *keys, *projected), outs)
 
 
 def merge(counts, queries, keys, own):
     rows = queries.shape[0]
     outs = [((HEADS, rows, rows), jnp.bfloat16)] * 2 + [((rows, PAIRS * LANES), jnp.float32)]
     outs += [((HEADS, rows, LANES), jnp.float32)] * 2
-    return call(merge_kernel, 0, (counts, queries, *keys, *own), outs)
+    return call(merge_kernel, (counts, queries, *keys, *own), outs)
 
 
 def collect(weights, values, sums, scales):
     outs = [((sums.shape[0], LANES), jnp.float32)]
-    return call(collect_kernel, -1, (*weights, *values, sums, scales), outs)[0]
+    return call(collect_kernel, (*weights, *values, sums, scales), outs)[0]
 
 
 def last_weights(counts, queries, keys, tops, totals):
     rows = queries.shape[0]
     outs = [((HEADS, rows, rows), jnp.bfloat16), ((PAIRS, rows, LANES), jnp.float32)]
-    return call(weights_kernel, 0, (counts, queries, keys, tops, totals), outs)
+    return call(weights_kernel, (counts, queries, keys, tops, totals), outs)
 
 
 def finish(shares, values, most, counts):
     outs = [((LATENT_CH, most.shape[0]), jnp.float32), ((1, LANES), jnp.float32)]
-    return call(finish_kernel, 3, (shares, values, most, counts), outs)
+    return call(finish_kernel, (shares, values, most, counts), outs)
 
 
 def exchange(shard, pairs):
@@ -272,6 +268,7 @@
     index = jnp.stack([own, partner, near, far, over])
     inside = (index >= 0) & (index < blocks)
     counts = jnp.where(inside, valid[jnp.clip(index, 0, blocks - 1)], 0).astype(jnp.int32)
+    counts = jnp.broadcast_to(counts[:, None], (len(index), LANES))
 
     keys_near = exchange(keys, near_pairs)
     keys_far = exchange(keys, far_pairs)
@@ -302,17 +299,18 @@
         for by in range(1, columns)
     ]
     squares = functools.reduce(jnp.add, moved, squares)
-    copies = jnp.broadcast_to(squares, (lax.axis_size(Z_CORE), LANES))
-    squares = exchanged_sum(copies, Z_CORE)[0, 0]
     count = jnp.float32(LATENT_CH) * jnp.sum(valid.astype(jnp.float32))
-    rms = jnp.sqrt(squares / count + 1e-06)
-    velocity = vel / rms
     level = timestep[0].astype(jnp.float32)
     early = 1.0 - level / STEPS
     later = 1.0 - (level + 1.0) / STEPS
     sigma_early = 5.0 * early / (1.0 + 4.0 * early)
     sigma_later = 5.0 * later / (1.0 + 4.0 * later)
-    return (velocity, latent + (sigma_later - sigma_early) * velocity)
+    copies = jnp.broadcast_to(squares, (lax.axis_size(Z_CORE), LANES))
+    copies, count, change = lax.optimization_barrier((copies, count, sigma_later - sigma_early))
+    squares = exchanged_sum(copies, Z_CORE)[0, 0]
+    rms = jnp.sqrt(squares / count + 1e-06)
+    velocity = vel / rms
+    return (velocity, latent + change * velocity)
 
 
 def solution(mesh):

time: 111 us -> 109 us (0.982)
  blocking collectives: 0 us -> 17.9 us
  waiting for transfers between devices: 29.1 us -> 17.7 us
  starting transfers between devices: 47.5 us -> 40.6 us
  Pallas kernels: 26.2 us -> 25 us
    all_to_all x0 -> x1, blocking collectives: none -> 17.9 us  [exchanged_sum(): gathered = lax.all_to_all(copies, axes, 0, 0, tiled=True)]
    all_to_all x1 -> x0, waiting for transfers between devices: 10.5 us -> none  [exchanged_sum(): gathered = lax.all_to_all(copies, axes, 0, 0, tiled=True)]
    all_to_all x1 -> x0, starting transfers between devices: 6.89 us -> none  [exchanged_sum(): gathered = lax.all_to_all(copies, axes, 0, 0, tiled=True)]
    pallas_call x6, Pallas kernels: 26.2 us -> 25 us  [call(): pl.pallas_call(kernel, in_specs=[here] * len(operands), out_specs=[here]...]
  transfers between devices with their start and end apart: 12 -> 11, of which waited for: 6 -> 5; matrix products, arithmetic and copies ran while one was open for 2% -> 2% of each run, Pallas kernels for 22% -> 22%
where the time goes in v4:
time: 109 us
  starting transfers between devices  40.6 us (37%)
  Pallas kernels  25 us (23%)
  blocking collectives  17.9 us (16%)
  waiting for transfers between devices  17.7 us (16%)
  local copies, waits for them, and re-layouts  3.98 us (4%)
  between operations  2.26 us (2%)
  other arithmetic  1.35 us (1%)
    ppermute x8, starting transfers between devices, exchange(): return lax.ppermute(shard, BLK, pairs)  39.1 us
    pallas_call x6, Pallas kernels, call(): pl.pallas_call(kernel, in_specs=[here] * len(operands), out_specs=[here]...  25 us
    all_to_all x1, blocking collectives, exchanged_sum(): gathered = lax.all_to_all(copies, axes, 0, 0, tiled=True)  17.9 us
    ppermute x8, waiting for transfers between devices, exchange(): return lax.ppermute(shard, BLK, pairs)  14.5 us
    ppermute x3, waiting for transfers between devices, step(): lax.ppermute(squares, 'blk_1', [(i, (i + by) % columns) for i in range(co...  3.18 us
    unnamed x12, local copies, waits for them, and re-layouts  2.32 us
  transfers between devices with their start and end apart: 11, of which 5 were waited for; matrix products, arithmetic and copies ran while one was open for 2% of the time, Pallas kernels for 22%

profile of v4, /device:TPU:33, one launch (start us, length us, event | category | flops | bytes accessed | tf_op | source)
XLA Modules:
  0.0 108.8 jit_solution(8186277793518702714)
XLA Ops:
  0.6 2.3 %collective-permute-start.1 = (bf16[256,2560]{1,0:T(8,128)(2,1)}, bf16[256,2560]{1,0:T(8,128)(2,1)S(1)}, u32[]{:S(2)}, u32[]{:S(2)}) collective-permute-start(bf16[256,2560]{1,0:T(8,128)(2,1)} %refs_0_.1), channel_id=1, source_target_pairs={{2,0},{127,1},{4,2},{1,3},{6,4},{3,5},{8,6},{5,7},{10,8},{7,9},{12... | collective-permute-start | bytes 3932168 | tf_op jit(solution)/shard_map/ppermute | solution.py:249
  2.9 24.2 %collective-permute-start.3 = (bf16[256,2560]{1,0:T(8,128)(2,1)}, bf16[256,2560]{1,0:T(8,128)(2,1)}, u32[]{:S(2)}, u32[]{:S(2)}) collective-permute-start(bf16[256,2560]{1,0:T(8,128)(2,1)} %refs_0_.1), channel_id=1, source_target_pairs={{0,1},{1,0},{2,3},{3,2},{4,5},{5,4},{6,7},{7,6},{8,9},{9,8},{10,11... | collective-permute-start | bytes 3932168 | tf_op jit(solution)/shard_map/ppermute | solution.py:249
  27.1 14.3 %collective-permute-done.1.refs_0_ = bf16[256,2560]{1,0:T(8,128)(2,1)S(1)} collective-permute-done((bf16[256,2560]{1,0:T(8,128)(2,1)}, bf16[256,2560]{1,0:T(8,128)(2,1)S(1)}, u32[]{:S(2)}, u32[]{:S(2)}) %collective-permute-start.1) | collective-permute-done | bytes 1310752 | tf_op jit(solution)/shard_map/ppermute | solution.py:249
  41.5 1.1 %collective-permute-start.2 = (bf16[256,2560]{1,0:T(8,128)(2,1)S(1)}, bf16[256,2560]{1,0:T(8,128)(2,1)}, u32[]{:S(2)}, u32[]{:S(2)}) collective-permute-start(bf16[256,2560]{1,0:T(8,128)(2,1)S(1)} %collective-permute-done.1.refs_0_), channel_id=1, source_target_pairs={{0,1},{1,0},{2,3},{3,2},{4,5},{5,4},{6,7},{7,6},{8,9},{9,8},{10,11... | collective-permute-start | bytes 3932168 | tf_op jit(solution)/shard_map/ppermute | solution.py:249
  42.7 1.4 %gather_fusion = s32[5]{0:T(128)S(1)} fusion(s32[128]{0:T(128)} %param.12, s32[1024]{0:T(1024)S(1)} %pad_clamp_fusion), kind=kCustom, calls=%fused_computation | custom fusion | bytes 60 | tf_op jit(solution)/shard_map/gather | solution.py:270
  44.3 1.3 %copy-done.1 = bf16[256,2560]{1,0:T(8,128)(2,1)S(1)} copy-done((bf16[256,2560]{1,0:T(8,128)(2,1)S(1)}, bf16[256,2560]{1,0:T(8,128)(2,1)}, u32[]{:S(2)}) %copy-start.1) | copy-done | bytes 1310744
  45.6 1.0 copy-done.3
  46.6 1.9 %shard_map.86.refs_2_ = bf16[256,1280]{1,0:T(8,128)(2,1)S(1)} custom-call(s32[5,128]{1,0:T(8,128)S(1)} %broadcast_in_dim.10.counts, bf16[256,2560]{1,0:T(8,128)(2,1)S(1)} %copy-done.1, bf16[64,2560]{1,0:T(8,128)(2,1)S(1)} %copy-done.3), custom_call_target="tpu_custom_call" | custom-call | tf_op jit(solution)/shard_map/pallas_call | solution.py:204
  48.5 0.1 collective-permute-start.4
  48.8 5.5 %collective-permute-start = (bf16[256,2560]{1,0:T(8,128)(2,1)S(1)}, bf16[256,2560]{1,0:T(8,128)(2,1)S(1)}, u32[]{:S(2)}, u32[]{:S(2)}) collective-permute-start(bf16[256,2560]{1,0:T(8,128)(2,1)S(1)} %copy-done.2), channel_id=1, source_target_pairs={{126,0},{3,1},{0,2},{5,3},{2,4},{7,5},{4,6},{9,7},{6,8},{11,9},{8,... | collective-permute-start | bytes 3932168 | tf_op jit(solution)/shard_map/ppermute | solution.py:249
  54.4 8.9 %shard_map.87 = (f32[256,1280]{1,0:T(8,128)S(1)}, f32[20,256,128]{2,1,0:T(8,128)S(1)}, f32[20,256,128]{2,1,0:T(8,128)S(1)}) custom-call(s32[5,128]{1,0:T(8,128)S(1)} %broadcast_in_dim.10.counts, bf16[256,2560]{1,0:T(8,128)(2,1)S(1)} %copy-done, bf16[256,2560]{1,0:T(8,128)(2,1)S(1)} %copy-done.2, bf16[256,2560]{1,0:T(8,128)(2,1)} %collective-permute-done.3.refs_1_, ...), custom_call_target="tpu_custom_call" | custom-call | tf_op jit(solution)/shard_map/pallas_call | solution.py:204
  63.3 7.0 %shard_map.88 = (bf16[20,256,256]{2,1,0:T(8,128)(2,1)S(1)}, bf16[20,256,256]{2,1,0:T(8,128)(2,1)S(1)}, f32[256,1280]{1,0:T(8,128)S(1)}, f32[20,256,128]{2,1,0:T(8,128)S(1)}, f32[20,256,128]{2,1,0:T(8,128)S(1)}) custom-call(s32[5,128]{1,0:T(8,128)S(1)} %broadcast_in_dim.10.counts, bf16[256,2560]{1,0:T(8,128)(2,1)S(1)} %copy-done, ...), custom_call_target="tpu_custom_call" | custom-call | tf_op jit(solution)/shard_map/pallas_call | solution.py:204
  70.3 0.6 collective-permute-start.7
  71.0 5.0 %collective-permute-start.5 = (bf16[256,1280]{1,0:T(8,128)(2,1)S(1)}, bf16[256,1280]{1,0:T(8,128)(2,1)S(1)}, u32[]{:S(2)}, u32[]{:S(2)}) collective-permute-start(bf16[256,1280]{1,0:T(8,128)(2,1)S(1)} %shard_map.86.refs_2_), channel_id=1, source_target_pairs={{126,0},{3,1},{0,2},{5,3},{2,4},{7,5},{4,6},{9,7},{6,8},{11,9},{8,... | collective-permute-start | bytes 1966088 | tf_op jit(solution)/shard_map/ppermute | solution.py:249
  76.7 0.6 convert_reduce_fusion
  77.3 4.5 %shard_map.89 = (bf16[20,256,256]{2,1,0:T(8,128)(2,1)S(1)}, f32[10,256,128]{2,1,0:T(8,128)S(1)}) custom-call(s32[5,128]{1,0:T(8,128)S(1)} %broadcast_in_dim.10.counts, bf16[256,2560]{1,0:T(8,128)(2,1)S(1)} %copy-done, bf16[256,2560]{1,0:T(8,128)(2,1)S(1)} %collective-permute-done.keys, f32[20,256,128]{2,1,0:T(8,128)S(1)} %get-tuple-element.25.tops, ...), custom_call_target="tpu_custom_call" | custom-call | tf_op jit(solution)/shard_map/pallas_call | solution.py:204
  81.8 1.6 %shard_map.90.most = f32[256,128]{1,0:T(8,128)S(1)} custom-call(bf16[20,256,256]{2,1,0:T(8,128)(2,1)S(1)} %get-tuple-element.29.near, bf16[20,256,256]{2,1,0:T(8,128)(2,1)S(1)} %get-tuple-element.30.over, bf16[256,1280]{1,0:T(8,128)(2,1)S(1)} %collective-permute-done.6.near_values, bf16[256,1280]{1,0:T(8,128)(2,1)S(1)} %collective-permute-done.7.over_values, ...), custom_call_target="tpu_custom_call" | custom-call | tf_op jit(solution)/shard_map/pallas_call | solution.py:204
  83.5 1.0 shard_map.91
  84.6 1.4 %collective-permute-start.8 = (f32[1,128]{1,0:T(1,128)S(1)}, f32[1,128]{1,0:T(1,128)S(1)}, u32[]{:S(2)}, u32[]{:S(2)}) collective-permute-start(f32[1,128]{1,0:T(1,128)S(1)} %get-tuple-element.36), channel_id=1, source_target_pairs={{0,2},{2,4},{4,6},{6,0},{1,3},{3,5},{5,7},{7,1},{8,10},{10,12},{12... | collective-permute-start | bytes 1544 | tf_op jit(solution)/shard_map/ppermute | solution.py:298
  86.8 0.2 collective-permute-done.10
  87.0 1.3 %collective-permute-done.8 = f32[1,128]{1,0:T(1,128)S(1)} collective-permute-done((f32[1,128]{1,0:T(1,128)S(1)}, f32[1,128]{1,0:T(1,128)S(1)}, u32[]{:S(2)}, u32[]{:S(2)}) %collective-permute-start.8) | collective-permute-done | bytes 544 | tf_op jit(solution)/shard_map/ppermute | solution.py:298
  88.4 1.6 %collective-permute-done.9 = f32[1,128]{1,0:T(1,128)S(1)} collective-permute-done((f32[1,128]{1,0:T(1,128)S(1)}, f32[1,128]{1,0:T(1,128)S(1)}, u32[]{:S(2)}, u32[]{:S(2)}) %collective-permute-start.9) | collective-permute-done | bytes 544 | tf_op jit(solution)/shard_map/ppermute | solution.py:298
  90.0 17.9 %all_to_all.9 = f32[32,1,128]{2,1,0:T(1,128)S(1)} all-to-all(f32[32,1,128]{2,1,0:T(1,128)S(1)} %bitcast.19), channel_id=1, replica_groups=mesh['groups'=2,'blk_0'=16,'blk_1'=4,'blk_2'=2] {'blk_0','blk_2'}, dimensions={0} | all-to-all | bytes 32768 | tf_op jit(solution)/shard_map/all_to_all | solution.py:253
  108.1 0.7 multiply_add_fusion
  (29 shorter events, 0.7 us)
Async XLA Ops:
  0.6 40.9 %collective-permute-start.1 = (bf16[256,2560]{1,0:T(8,128)(2,1)}, bf16[256,2560]{1,0:T(8,128)(2,1)S(1)}, u32[]{:S(2)}, u32[]{:S(2)}) collective-permute-start(bf16[256,2560]{1,0:T(8,128)(2,1)} %refs_0_.1), channel_id=1, source_target_pairs={{2,0},{127,1},{4,2},{1,3},{6,4},{3,5},{8,6},{5,7},{10,8},{7,9},{12... | collective-permute-start | bytes 3932168 | tf_op jit(solution)/shard_map/ppermute | solution.py:249
  2.9 51.5 %collective-permute-start.3 = (bf16[256,2560]{1,0:T(8,128)(2,1)}, bf16[256,2560]{1,0:T(8,128)(2,1)}, u32[]{:S(2)}, u32[]{:S(2)}) collective-permute-start(bf16[256,2560]{1,0:T(8,128)(2,1)} %refs_0_.1), channel_id=1, source_target_pairs={{0,1},{1,0},{2,3},{3,2},{4,5},{5,4},{6,7},{7,6},{8,9},{9,8},{10,11... | collective-permute-start | bytes 3932168 | tf_op jit(solution)/shard_map/ppermute | solution.py:249
  41.5 21.8 %collective-permute-start.2 = (bf16[256,2560]{1,0:T(8,128)(2,1)S(1)}, bf16[256,2560]{1,0:T(8,128)(2,1)}, u32[]{:S(2)}, u32[]{:S(2)}) collective-permute-start(bf16[256,2560]{1,0:T(8,128)(2,1)S(1)} %collective-permute-done.1.refs_0_), channel_id=1, source_target_pairs={{0,1},{1,0},{2,3},{3,2},{4,5},{5,4},{6,7},{7,6},{8,9},{9,8},{10,11... | collective-permute-start | bytes 3932168 | tf_op jit(solution)/shard_map/ppermute | solution.py:249
  42.7 11.7 %copy-start = (bf16[256,2560]{1,0:T(8,128)(2,1)S(1)}, bf16[256,2560]{1,0:T(8,128)(2,1)}, u32[]{:S(2)}) copy-start(bf16[256,2560]{1,0:T(8,128)(2,1)} %queries.5) | copy-start | bytes 3932164
  44.3 1.3 %copy-start.1 = (bf16[256,2560]{1,0:T(8,128)(2,1)S(1)}, bf16[256,2560]{1,0:T(8,128)(2,1)}, u32[]{:S(2)}) copy-start(bf16[256,2560]{1,0:T(8,128)(2,1)} %values.1) | copy-start | bytes 3932164
  45.6 1.0 copy-start.3
  46.6 2.2 %copy-start.2 = (bf16[256,2560]{1,0:T(8,128)(2,1)S(1)}, bf16[256,2560]{1,0:T(8,128)(2,1)}, u32[]{:S(2)}) copy-start(bf16[256,2560]{1,0:T(8,128)(2,1)} %refs_0_.1) | copy-start | bytes 3932164
  48.5 5.8 %collective-permute-start.4 = (bf16[256,1280]{1,0:T(8,128)(2,1)S(1)}, bf16[256,1280]{1,0:T(8,128)(2,1)S(1)}, u32[]{:S(2)}, u32[]{:S(2)}) collective-permute-start(bf16[256,1280]{1,0:T(8,128)(2,1)S(1)} %shard_map.86.refs_2_), channel_id=1, source_target_pairs={{0,1},{1,0},{2,3},{3,2},{4,5},{5,4},{6,7},{7,6},{8,9},{9,8},{10,11... | collective-permute-start | bytes 1966088 | tf_op jit(solution)/shard_map/ppermute | solution.py:249
  48.7 21.6 %collective-permute-start.6 = (bf16[256,1280]{1,0:T(8,128)(2,1)S(1)}, bf16[256,1280]{1,0:T(8,128)(2,1)S(1)}, u32[]{:S(2)}, u32[]{:S(2)}) collective-permute-start(bf16[256,1280]{1,0:T(8,128)(2,1)S(1)} %shard_map.86.refs_2_), channel_id=1, source_target_pairs={{2,0},{127,1},{4,2},{1,3},{6,4},{3,5},{8,6},{5,7},{10,8},{7,9},{12... | collective-permute-start | bytes 1966088 | tf_op jit(solution)/shard_map/ppermute | solution.py:249
  48.8 28.5 %collective-permute-start = (bf16[256,2560]{1,0:T(8,128)(2,1)S(1)}, bf16[256,2560]{1,0:T(8,128)(2,1)S(1)}, u32[]{:S(2)}, u32[]{:S(2)}) collective-permute-start(bf16[256,2560]{1,0:T(8,128)(2,1)S(1)} %copy-done.2), channel_id=1, source_target_pairs={{126,0},{3,1},{0,2},{5,3},{2,4},{7,5},{4,6},{9,7},{6,8},{11,9},{8,... | collective-permute-start | bytes 3932168 | tf_op jit(solution)/shard_map/ppermute | solution.py:249
  63.3 13.4 %copy-start.4 = (s32[128]{0:T(128)S(1)}, s32[128]{0:T(128)}, u32[]{:S(2)}) copy-start(s32[128]{0:T(128)} %param.12) | copy-start | bytes 1540
  70.3 11.5 %collective-permute-start.7 = (bf16[256,1280]{1,0:T(8,128)(2,1)S(1)}, bf16[256,1280]{1,0:T(8,128)(2,1)S(1)}, u32[]{:S(2)}, u32[]{:S(2)}) collective-permute-start(bf16[256,1280]{1,0:T(8,128)(2,1)S(1)} %collective-permute-done.6.near_values), channel_id=1, source_target_pairs={{0,1},{1,0},{2,3},{3,2},{4,5},{5,4},{6,7},{7,6},{8,9},{9,8},{10,11... | collective-permute-start | bytes 1966088 | tf_op jit(solution)/shard_map/ppermute | solution.py:249
  71.0 12.6 %collective-permute-start.5 = (bf16[256,1280]{1,0:T(8,128)(2,1)S(1)}, bf16[256,1280]{1,0:T(8,128)(2,1)S(1)}, u32[]{:S(2)}, u32[]{:S(2)}) collective-permute-start(bf16[256,1280]{1,0:T(8,128)(2,1)S(1)} %shard_map.86.refs_2_), channel_id=1, source_target_pairs={{126,0},{3,1},{0,2},{5,3},{2,4},{7,5},{4,6},{9,7},{6,8},{11,9},{8,... | collective-permute-start | bytes 1966088 | tf_op jit(solution)/shard_map/ppermute | solution.py:249
  83.5 24.6 %copy-start.5 = (f32[64,256]{1,0:T(8,128)S(1)}, f32[64,256]{1,0:T(8,128)}, u32[]{:S(2)}) copy-start(f32[64,256]{1,0:T(8,128)} %param.11) | copy-start | bytes 196612
  84.6 2.5 %collective-permute-start.10 = (f32[1,128]{1,0:T(1,128)S(1)}, f32[1,128]{1,0:T(1,128)S(1)}, u32[]{:S(2)}, u32[]{:S(2)}) collective-permute-start(f32[1,128]{1,0:T(1,128)S(1)} %get-tuple-element.36), channel_id=1, source_target_pairs={{0,6},{2,0},{4,2},{6,4},{1,7},{3,1},{5,3},{7,5},{8,14},{10,8},{12,... | collective-permute-start | bytes 1544 | tf_op jit(solution)/shard_map/ppermute | solution.py:298
  84.6 3.7 %collective-permute-start.8 = (f32[1,128]{1,0:T(1,128)S(1)}, f32[1,128]{1,0:T(1,128)S(1)}, u32[]{:S(2)}, u32[]{:S(2)}) collective-permute-start(f32[1,128]{1,0:T(1,128)S(1)} %get-tuple-element.36), channel_id=1, source_target_pairs={{0,2},{2,4},{4,6},{6,0},{1,3},{3,5},{5,7},{7,1},{8,10},{10,12},{12... | collective-permute-start | bytes 1544 | tf_op jit(solution)/shard_map/ppermute | solution.py:298
  86.1 3.9 %collective-permute-start.9 = (f32[1,128]{1,0:T(1,128)S(1)}, f32[1,128]{1,0:T(1,128)S(1)}, u32[]{:S(2)}, u32[]{:S(2)}) collective-permute-start(f32[1,128]{1,0:T(1,128)S(1)} %get-tuple-element.36), channel_id=1, source_target_pairs={{0,4},{2,6},{4,0},{6,2},{1,5},{3,7},{5,1},{7,3},{8,12},{10,14},{12... | collective-permute-start | bytes 1544 | tf_op jit(solution)/shard_map/ppermute | solution.py:298
